TPU v7x, 16 devices: a whole 2x2x2 slice. The times are simulated.
16 devices in a mesh: tp: 2 (over z), fsdp: 8 (over y, x, core).
Axes of the slice: x: 2, y: 2, z: 2, core: 2. Of those that a mesh axis runs over, the one named last changes fastest.
Arguments:
- x_act: bfloat16 [128, 256, 3072], P('fsdp', 'tp')
- rms_gain: float32 [3072], replicated
- w_query: bfloat16 [3072, 3072], P('fsdp', 'tp')
- w_key: bfloat16 [3072, 1024], P('fsdp', 'tp')
- w_value: bfloat16 [3072, 1024], P('fsdp', 'tp')
- w_out: bfloat16 [3072, 3072], P('tp', 'fsdp')
- dy_out: bfloat16 [128, 256, 3072], P('fsdp', 'tp')
Outputs:
- output 1: bfloat16 [128, 256, 3072], P('fsdp', 'tp')
- output 2: bfloat16 [128, 256, 3072], P('fsdp', 'tp')
- output 3: bfloat16 [3072, 3072], P('fsdp', 'tp')
- output 4: bfloat16 [3072, 1024], P('fsdp', 'tp')
- output 5: bfloat16 [3072, 1024], P('fsdp', 'tp')
- output 6: bfloat16 [3072, 3072], P('tp', 'fsdp')
- output 7: float32 [3072], replicated
All inputs are finite; a program needn't handle non-finite values.
Results may differ from a plain program's by a relative error of at most 0.0184875.
Values are sent between devices in bfloat16 or wider.
A program may use at most 1 GiB of HBM per device.

v0:
```python
import jax
import jax.numpy as jnp
from jax import lax
from jax.sharding import PartitionSpec as P

HEAD_DIM = 128
NORM_EPS = 1e-5
ROPE_THETA = 5.0e5
INV_FREQ = tuple(ROPE_THETA ** (-2.0 * pair_idx / HEAD_DIM) for pair_idx in range(HEAD_DIM // 2))


def rope_tables(seq_len):
    positions = jnp.arange(seq_len, dtype=jnp.float32)
    angles = positions[:, None] * jnp.asarray(INV_FREQ, dtype=jnp.float32)[None, :]
    return jnp.cos(angles), jnp.sin(angles)


def rotate(head_vals, cos_tab, sin_tab, direction):
    half_dim = HEAD_DIM // 2
    vals_f = head_vals.astype(jnp.float32)
    first_half = vals_f[..., :half_dim]
    second_half = vals_f[..., half_dim:]
    cos_b = cos_tab[:, None, :]
    sin_b = direction * sin_tab[:, None, :]
    return jnp.concatenate([first_half * cos_b - second_half * sin_b, second_half * cos_b + first_half * sin_b], axis=-1)


def solution(mesh):
    tp_size = mesh.shape['tp']
    acc_type = jnp.float32
    low_type = jnp.bfloat16
    act_spec = P('fsdp', 'tp', None)
    col_spec = P('fsdp', 'tp')
    row_spec = P('tp', 'fsdp')

    def shard_body(x_loc, rms_gain, wq_loc, wk_loc, wv_loc, wo_loc, dy_loc):
        batch_loc = x_loc.shape[0]
        seq_loc = x_loc.shape[1]
        seq_len = seq_loc * tp_size
        q_cols = wq_loc.shape[1]
        hq_loc = q_cols // HEAD_DIM
        kv_heads = wk_loc.shape[1] * tp_size // HEAD_DIM
        kv_loc = max(1, kv_heads // tp_size)
        group_loc = hq_loc // kv_loc
        kv_cols = kv_loc * HEAD_DIM
        replicated_kv = tp_size > kv_heads
        score_scale = HEAD_DIM ** -0.5

        wq_full = lax.all_gather(wq_loc, 'fsdp', axis=0, tiled=True)
        wk_full = lax.all_gather(wk_loc, 'fsdp', axis=0, tiled=True)
        wv_full = lax.all_gather(wv_loc, 'fsdp', axis=0, tiled=True)
        wo_full = lax.all_gather(wo_loc, 'fsdp', axis=1, tiled=True)
        if replicated_kv:
            kv_head = lax.axis_index('tp') // (tp_size // kv_heads)
            wk_full = lax.dynamic_slice_in_dim(lax.all_gather(wk_full, 'tp', axis=1, tiled=True), kv_head * HEAD_DIM, HEAD_DIM, axis=1)
            wv_full = lax.dynamic_slice_in_dim(lax.all_gather(wv_full, 'tp', axis=1, tiled=True), kv_head * HEAD_DIM, HEAD_DIM, axis=1)

        x_f = x_loc.astype(acc_type)
        inv_rms = lax.rsqrt(jnp.mean(x_f * x_f, axis=-1, keepdims=True) + NORM_EPS)
        normed = lax.all_gather((x_f * inv_rms * rms_gain).astype(low_type), 'tp', axis=1, tiled=True)
        cos_tab, sin_tab = rope_tables(seq_len)
        q_proj = jnp.einsum('bsd,dj->bsj', normed, wq_full, preferred_element_type=acc_type).astype(low_type)
        k_proj = jnp.einsum('bsd,dj->bsj', normed, wk_full, preferred_element_type=acc_type).astype(low_type)
        values = jnp.einsum('bsd,dj->bsj', normed, wv_full, preferred_element_type=acc_type).astype(low_type)
        values = values.reshape(batch_loc, seq_len, kv_loc, HEAD_DIM)
        queries = rotate(q_proj.reshape(batch_loc, seq_len, hq_loc, HEAD_DIM), cos_tab, sin_tab, 1.0).astype(low_type)
        queries = queries.reshape(batch_loc, seq_len, kv_loc, group_loc, HEAD_DIM)
        keys_rot = rotate(k_proj.reshape(batch_loc, seq_len, kv_loc, HEAD_DIM), cos_tab, sin_tab, 1.0).astype(low_type)
        causal = jnp.arange(seq_len)[:, None] >= jnp.arange(seq_len)[None, :]
        scores = jnp.einsum('bqcgd,bkcd->bcgqk', queries, keys_rot, preferred_element_type=acc_type) * score_scale
        attn_prob = jax.nn.softmax(jnp.where(causal, scores, -1e30), axis=-1)
        attn_prob_bf = attn_prob.astype(low_type)
        attn_mixed = jnp.einsum('bcgqk,bkcd->bqcgd', attn_prob_bf, values, preferred_element_type=acc_type).astype(low_type)
        attn_mixed = attn_mixed.reshape(batch_loc, seq_len, q_cols)
        out_part = jnp.einsum('bsj,jd->bsd', attn_mixed, wo_full, preferred_element_type=acc_type).astype(low_type)
        out_loc = lax.psum_scatter(out_part, 'tp', scatter_dimension=1, tiled=True)
        y_loc = (x_f + out_loc.astype(acc_type)).astype(low_type)

        dy_full = lax.all_gather(dy_loc, 'tp', axis=1, tiled=True)
        d_mixed = jnp.einsum('bsd,jd->bsj', dy_full, wo_full, preferred_element_type=acc_type).astype(low_type)
        d_mixed = d_mixed.reshape(batch_loc, seq_len, kv_loc, group_loc, HEAD_DIM)
        dwo_part = jnp.einsum('bsj,bsd->jd', attn_mixed, dy_full, preferred_element_type=acc_type)
        d_values = jnp.einsum('bcgqk,bqcgd->bkcd', attn_prob_bf, d_mixed, preferred_element_type=acc_type).astype(low_type)
        d_values = d_values.reshape(batch_loc, seq_len, kv_cols)
        d_prob = jnp.einsum('bqcgd,bkcd->bcgqk', d_mixed, values, preferred_element_type=acc_type)
        d_scores = attn_prob * (d_prob - jnp.sum(attn_prob * d_prob, axis=-1, keepdims=True))
        d_scores_bf = (d_scores * score_scale).astype(low_type)
        d_q_rot = jnp.einsum('bcgqk,bkcd->bqcgd', d_scores_bf, keys_rot, preferred_element_type=acc_type)
        d_k_rot = jnp.einsum('bcgqk,bqcgd->bkcd', d_scores_bf, queries, preferred_element_type=acc_type)
        d_queries = rotate(d_q_rot.reshape(batch_loc, seq_len, hq_loc, HEAD_DIM), cos_tab, sin_tab, -1.0).astype(low_type)
        d_queries = d_queries.reshape(batch_loc, seq_len, q_cols)
        d_keys = rotate(d_k_rot, cos_tab, sin_tab, -1.0).astype(low_type).reshape(batch_loc, seq_len, kv_cols)
        dwq_part = jnp.einsum('bsd,bsj->dj', normed, d_queries, preferred_element_type=acc_type)
        dwk_part = jnp.einsum('bsd,bsj->dj', normed, d_keys, preferred_element_type=acc_type)
        dwv_part = jnp.einsum('bsd,bsj->dj', normed, d_values, preferred_element_type=acc_type)
        d_normed_part = (jnp.einsum('bsj,dj->bsd', d_queries, wq_full, preferred_element_type=acc_type)
                         + jnp.einsum('bsj,dj->bsd', d_keys, wk_full, preferred_element_type=acc_type)
                         + jnp.einsum('bsj,dj->bsd', d_values, wv_full, preferred_element_type=acc_type)).astype(low_type)
        d_normed = lax.psum_scatter(d_normed_part, 'tp', scatter_dimension=1, tiled=True).astype(acc_type)

        grad_gain = d_normed * rms_gain
        d_gain = lax.psum(jnp.sum(d_normed * x_f * inv_rms, axis=(0, 1)), ('tp', 'fsdp'))
        mean_gx = jnp.mean(grad_gain * x_f, axis=-1, keepdims=True)
        dx_loc = (dy_loc.astype(acc_type) + inv_rms * (grad_gain - x_f * inv_rms * inv_rms * mean_gx)).astype(low_type)

        dwq_loc = lax.psum_scatter(dwq_part, 'fsdp', scatter_dimension=0, tiled=True)
        dwk_loc = lax.psum_scatter(dwk_part, 'fsdp', scatter_dimension=0, tiled=True)
        dwv_loc = lax.psum_scatter(dwv_part, 'fsdp', scatter_dimension=0, tiled=True)
        dwo_loc = lax.psum_scatter(dwo_part, 'fsdp', scatter_dimension=1, tiled=True)
        if replicated_kv:
            zero_cols = jnp.zeros((dwk_loc.shape[0], kv_heads * HEAD_DIM), acc_type)
            dwk_loc = lax.psum_scatter(lax.dynamic_update_slice(zero_cols, dwk_loc, (0, kv_head * HEAD_DIM)), 'tp', scatter_dimension=1, tiled=True)
            dwv_loc = lax.psum_scatter(lax.dynamic_update_slice(zero_cols, dwv_loc, (0, kv_head * HEAD_DIM)), 'tp', scatter_dimension=1, tiled=True)
        return (y_loc, dx_loc, dwq_loc.astype(low_type), dwk_loc.astype(low_type), dwv_loc.astype(low_type),
                dwo_loc.astype(low_type), d_gain)

    return jax.shard_map(shard_body, mesh=mesh,
                         in_specs=(act_spec, P(), col_spec, col_spec, col_spec, row_spec, act_spec),
                         out_specs=(act_spec, act_spec, col_spec, col_spec, col_spec, row_spec, P()),
                         check_vma=False)
```

profile of v0, /device:TPU:0, one launch (start us, length us, event | category | flops | bytes accessed | tf_op | source)
XLA Modules:
  0.0 2082.0 jit_solution(10808786569473541910)
XLA Ops:
  41.1 295.8 %all-gather.7.cloned.1.call-done = bf16[16,256,3072]{2,1,0:T(8,128)(2,1)} async-done(((bf16[16,128,3072]{2,1,0:T(8,128)(2,1)}), bf16[16,256,3072]{2,1,0:T(8,128)(2,1)}) %all-gather.7.cloned.1.call-update) | async-done | bytes 25165840 | tf_op jit(solution)/shard_map/all_gather | solution.py:60
  336.9 20.9 %fusion.55 = bf16[16,256,512]{2,1,0:T(8,128)(2,1)} fusion(bf16[16,256,3072]{2,1,0:T(8,128)(2,1)} %all-gather.7.cloned.1.call-done, bf16[3072,512]{1,0:T(8,128)(2,1)} %all-gather.9.cloned.1.call-done), kind=kOutput, calls=%fused_computation.81 | convolution fusion | flops 12886999040 | bytes 32505856 | tf_op jit(solution)/shard_map/bsd,dj->bsj/dot_general | solution.py:64
  367.2 20.9 %convert_convert_fusion = f32[16,256,512]{2,1,0:T(8,128)} fusion(bf16[16,256,3072]{2,1,0:T(8,128)(2,1)} %all-gather.7.cloned.1.call-done, bf16[3072,512]{1,0:T(8,128)(2,1)} %all-gather.11.cloned.1.call-done), kind=kOutput, calls=%fused_computation.67 | convolution fusion | flops 12889096192 | bytes 36700160 | tf_op jit(solution)/shard_map/bsd,dj->bsj/dot_general | solution.py:63
  398.3 27.4 %all-gather.15.cloned.1.call-done = bf16[1536,3072]{1,0:T(8,128)(2,1)} async-done(((bf16[1536,384]{1,0:T(8,128)(2,1)}), bf16[1536,3072]{1,0:T(8,128)(2,1)}) %all-gather.15.cloned.1.call-update) | async-done | bytes 9437200 | tf_op jit(solution)/shard_map/all_gather | solution.py:52
  425.7 295.1 %all-gather.17.cloned.1.call-done = bf16[16,256,3072]{2,1,0:T(8,128)(2,1)} async-done(((bf16[16,128,3072]{2,1,0:T(8,128)(2,1)}), bf16[16,256,3072]{2,1,0:T(8,128)(2,1)}) %all-gather.17.cloned.1.call-update) | async-done | bytes 25165840 | tf_op jit(solution)/shard_map/all_gather | solution.py:79
  720.8 46.9 %convolution_convert_fusion.1 = bf16[16,256,1536]{2,1,0:T(8,128)(2,1)} fusion(bf16[16,256,3072]{2,1,0:T(8,128)(2,1)} %all-gather.17.cloned.1.call-done, bf16[1536,3072]{1,0:T(8,128)(2,1)} %all-gather.15.cloned.1.call-done), kind=kOutput, calls=%fused_computation.38 | convolution fusion | flops 38660997120 | bytes 47185920 | tf_op jit(solution)/shard_map/bsd,jd->bsj/dot_general | solution.py:80
  767.7 16.6 copy.78
  784.3 14.2 fusion.66
  798.5 48.0 %fusion.25 = f32[16,256,1536]{2,1,0:T(8,128)} fusion(bf16[16,256,3072]{2,1,0:T(8,128)(2,1)} %all-gather.7.cloned.1.call-done, bf16[3072,1536]{1,0:T(8,128)(2,1)} %all-gather.13.cloned.1.call-done), kind=kOutput, calls=%fused_computation.40 | convolution fusion | flops 38667288576 | bytes 59768832 | tf_op jit(solution)/shard_map/bsd,dj->bsj/dot_general | solution.py:62
  846.5 24.7 %copy.72 = f32[16,256,1536]{1,2,0:T(8,128)} copy(f32[16,256,1536]{2,1,0:T(8,128)} %fusion.25) | data formatting | bytes 50331648 | tf_op jit(solution)/shard_map/convert_element_type | solution.py:20
  871.2 15.1 subtract_convert_fusion.1
  886.3 12.1 copy.73
  898.4 12.0 copy.74
  910.4 23.0 %fusion.40 = f32[16,4,256,256,3]{3,2,4,1,0:T(8,128)} fusion(bf16[16,256,4,3,128]{1,4,3,2,0:T(8,128)(2,1)} %bitcast.135, bf16[16,256,4,128,1]{3,2,1,0,4:T(4,128)(2,1)} %bitcast.138), kind=kOutput, calls=%fused_computation.70 | convolution fusion | flops 3221225472 | bytes 67108864 | tf_op jit(solution)/shard_map/bqcgd,bkcd->bcgqk/dot_general | solution.py:85
  944.0 35.9 %fusion.67 = (f32[16,4,3,256]{3,2,1,0:T(4,128)S(1)}, f32[16,4,3,256,256]{3,4,2,1,0:T(8,128)}) fusion(pred[256,256]{0,1:T(8,128)(4,1)S(1)} %copy-done.14, bf16[16,256,4,64]{3,1,2,0:T(8,128)(2,1)} %get-tuple-element.14, bf16[16,256,4,64]{3,1,2,0:T(8,128)(2,1)} %get-tuple-element.13, bf16[16,256,4,3,64]{4,1,3,2,0:T(8,128)(2,1)} %bitcast.144, ...), kind=kOutput, calls=%fused_computation.96 | convolution fusion | flops 3305111808 | bytes 67371008 | tf_op jit(solution)/shard_map/sub | solution.py:71
  979.9 72.1 %fusion.44 = f32[16,256,4,128]{3,1,2,0:T(8,128)} fusion(f32[16,4,256,256,3]{3,2,4,1,0:T(8,128)} %fusion.40, bf16[16,256,4,3,64]{4,1,3,2,0:T(8,128)(2,1)} %bitcast.145, bf16[16,256,4,3,64]{4,1,3,2,0:T(8,128)(2,1)} %bitcast.143, f32[16,4,3,256,256]{3,4,2,1,0:T(8,128)} %get-tuple-element.25, f32[16,4,3,256]{3,2,1,0:T(4,128)S(1)} %get-tuple-element.24), kind=kOutput, calls=%fused_computation.72 | convolution fusion | flops 3334521088 | bytes 121831424 | tf_op jit(solution)/shard_map/bcgqk,bqcgd->bkcd/dot_general | solution.py:89
  1069.6 19.6 convolution_bitcast_fusion.3
  1089.3 27.3 %bitcast_convert_fusion = bf16[16,4,128,256]{3,2,1,0:T(8,128)(2,1)} fusion(bf16[16,256,4,3,128]{1,4,3,2,0:T(8,128)(2,1)} %bitcast.136, f32[16,4,3,256,256]{3,4,2,1,0:T(8,128)} %get-tuple-element.25, f32[16,4,3,256]{3,2,1,0:T(4,128)S(1)} %get-tuple-element.24), kind=kOutput, calls=%fused_computation.57 | convolution fusion | flops 3248488448 | bytes 67305472 | tf_op jit(solution)/shard_map/bcgqk,bqcgd->bkcd/dot_general | solution.py:83
  1116.6 19.7 convolution_bitcast_fusion.2
  1136.3 25.2 %fusion.34 = bf16[16,4,128,3,256]{4,2,3,1,0:T(8,128)(2,1)} fusion(bf16[16,256,4,128,1]{3,2,1,0,4:T(4,128)(2,1)} %bitcast.139, f32[16,4,3,256,256]{3,4,2,1,0:T(8,128)} %get-tuple-element.25, f32[16,4,3,256]{3,2,1,0:T(4,128)S(1)} %get-tuple-element.24), kind=kOutput, calls=%fused_computation.62 | convolution fusion | flops 3252682752 | bytes 67305472 | tf_op jit(solution)/shard_map/bcgqk,bkcd->bqcgd/dot_general | solution.py:73
  1161.5 48.8 %convolution_bitcast_fusion = f32[1536,3072]{1,0:T(8,128)} fusion(bf16[16,256,1536]{1,2,0:T(8,128)(2,1)} %bitcast.148, bf16[16,256,3072]{2,1,0:T(8,128)(2,1)} %all-gather.17.cloned.1.call-done), kind=kOutput, calls=%fused_computation.41 | convolution fusion | flops 38654705664 | bytes 56623104 | tf_op jit(solution)/shard_map/bsj,bsd->jd/dot_general | solution.py:82
  1210.4 86.3 %fusion.24 = f32[16,4,128,3,256]{4,2,3,1,0:T(8,128)} fusion(f32[16,4,256,256,3]{3,2,4,1,0:T(8,128)} %fusion.40, bf16[16,256,4,64]{3,1,2,0:T(8,128)(2,1)} %get-tuple-element.14, bf16[16,256,4,64]{3,1,2,0:T(8,128)(2,1)} %get-tuple-element.13, f32[16,4,3,256,256]{3,4,2,1,0:T(8,128)} %get-tuple-element.25, f32[16,4,3,256]{3,2,1,0:T(4,128)S(1)} %get-tuple-element.24), kind=kOutput, calls=%fused_computation.36 | convolution fusion | flops 3317743872 | bytes 130220032 | tf_op jit(solution)/shard_map/bcgqk,bkcd->bqcgd/dot_general | solution.py:88
  1312.8 49.0 %convolution_bitcast_fusion.1 = f32[3072,1536]{1,0:T(8,128)} fusion(bf16[16,256,3072]{2,1,0:T(8,128)(2,1)} %all-gather.7.cloned.1.call-done, bf16[16,256,1536]{1,2,0:T(8,128)(2,1)} %bitcast.140), kind=kOutput, calls=%fused_computation.42 | convolution fusion | flops 38654705664 | bytes 56623104 | tf_op jit(solution)/shard_map/bsd,bsj->dj/dot_general | solution.py:93
  1363.8 30.8 %fusion.51 = f32[16,256,3072]{2,1,0:T(8,128)} fusion(bf16[16,256,512]{1,2,0:T(8,128)(2,1)} %bitcast.151, bf16[3072,512]{1,0:T(8,128)(2,1)S(1)} %copy-done.16), kind=kOutput, calls=%fused_computation.77 | convolution fusion | flops 12884901888 | bytes 57671680 | tf_op jit(solution)/shard_map/bsj,dj->bsd/dot_general | solution.py:98
  1394.5 27.9 %fusion.45 = f32[16,256,3072]{2,1,0:T(8,128)} fusion(bf16[16,256,512]{1,2,0:T(8,128)(2,1)} %bitcast.147, bf16[3072,512]{1,0:T(8,128)(2,1)} %all-gather.11.cloned.1.call-done), kind=kOutput, calls=%fused_computation.73 | convolution fusion | flops 12884901888 | bytes 57671680 | tf_op jit(solution)/shard_map/bsj,dj->bsd/dot_general | solution.py:97
  1422.5 67.4 %add_convert_fusion = bf16[16,256,3072]{2,1,0:T(8,128)(2,1)} fusion(f32[16,256,3072]{2,1,0:T(8,128)} %fusion.51, f32[16,256,3072]{2,1,0:T(8,128)} %fusion.45, bf16[16,256,1536]{1,2,0:T(8,128)(2,1)} %bitcast.141, bf16[3072,1536]{1,0:T(8,128)(2,1)} %all-gather.13.cloned.1.call-done), kind=kOutput, calls=%fused_computation.8 | convolution fusion | flops 38692454400 | bytes 147849216 | tf_op jit(solution)/shard_map/bsj,dj->bsd/dot_general | solution.py:96
  1490.0 48.1 %convolution_convert_fusion = bf16[16,256,3072]{2,1,0:T(8,128)(2,1)} fusion(bf16[16,256,1536]{1,2,0:T(8,128)(2,1)} %bitcast.149, bf16[1536,3072]{1,0:T(8,128)(2,1)} %all-gather.15.cloned.1.call-done), kind=kOutput, calls=%fused_computation.37 | convolution fusion | flops 38667288576 | bytes 47185920 | tf_op jit(solution)/shard_map/bsj,jd->bsd/dot_general | solution.py:75
  1547.6 219.4 %reduce-scatter.9.cloned.1.call-done = bf16[16,128,3072]{2,1,0:T(8,128)(2,1)} async-done(((bf16[16,256,3072]{2,1,0:T(8,128)(2,1)}), bf16[16,128,3072]{2,1,0:T(8,128)(2,1)}) %reduce-scatter.9.cloned.1.call-update) | async-done | bytes 12582928 | tf_op jit(solution)/shard_map/reduce_scatter | solution.py:99
  1767.0 14.5 fusion.18
  1781.5 33.6 %psum.7 = f32[3072]{0:T(1024)} all-reduce(f32[3072]{0:T(1024)S(1)} %get-tuple-element.7), channel_id=1, replica_groups=mesh['tp'=2,'fsdp'=8] {'tp','fsdp'}, use_global_device_ids=true, to_apply=%region_12.13 | all-reduce | flops 3072 | bytes 24576 | tf_op jit(solution)/shard_map/psum | solution.py:102
  1815.1 233.1 %reduce-scatter.7.cloned.1.call-done = bf16[16,128,3072]{2,1,0:T(8,128)(2,1)} async-done(((bf16[16,256,3072]{2,1,0:T(8,128)(2,1)}), bf16[16,128,3072]{2,1,0:T(8,128)(2,1)}) %reduce-scatter.7.cloned.1.call-update) | async-done | bytes 12582928 | tf_op jit(solution)/shard_map/reduce_scatter | solution.py:76
  2048.2 26.7 %fusion.13 = (bf16[16,128,3072]{2,1,0:T(8,128)(2,1)}, bf16[16,128,3072]{2,1,0:T(8,128)(2,1)}) fusion(bf16[16,128,3072]{2,1,0:T(8,128)(2,1)} %param.8, bf16[16,128,3072]{2,1,0:T(8,128)(2,1)} %reduce-scatter.9.cloned.1.call-done, bf16[16,128,3072]{2,1,0:T(8,128)(2,1)} %param.14, f32[16,128]{1,0:T(8,128)S(1)} %broadcast_multiply_fusion.1, ...), kind=kLoop, calls=%fused_computation.24 | loop fusion | flops 88080384 | bytes 75526144 | tf_op jit(solution)/shard_map/convert_element_type | solution.py:104
  (86 shorter events, 109.4 us)
Async XLA Ops:
  7.2 8.5 copy-start.12
  7.2 33.9 %all-gather.9.cloned.1.call-start = ((), (), s32[]{:S(2)}) async-start(), calls=%async_computation.7 | async-start | bytes 3538944 | tf_op jit(solution)/shard_map/all_gather | solution.py:51
  7.9 329.0 %all-gather.7.cloned.1.call-start = ((), (), s32[]{:S(2)}) async-start(), calls=%async_computation.6 | async-start | bytes 37748736 | tf_op jit(solution)/shard_map/all_gather | solution.py:60
  15.1 0.6 copy-start.10
  27.2 2.6 copy-start.15
  27.3 339.9 %all-gather.11.cloned.1.call-start = ((), (), s32[]{:S(2)}) async-start(), calls=%async_computation.8 | async-start | bytes 3538944 | tf_op jit(solution)/shard_map/all_gather | solution.py:50
  28.0 397.7 %all-gather.15.cloned.1.call-start = ((), (), s32[]{:S(2)}) async-start(), calls=%async_computation.10 | async-start | bytes 10616832 | tf_op jit(solution)/shard_map/all_gather | solution.py:52
  28.6 692.2 %all-gather.17.cloned.1.call-start = ((), (), s32[]{:S(2)}) async-start(), calls=%async_computation.12 | async-start | bytes 37748736 | tf_op jit(solution)/shard_map/all_gather | solution.py:79
  29.2 769.3 %all-gather.13.cloned.1.call-start = ((), (), s32[]{:S(2)}) async-start(), calls=%async_computation.9 | async-start | bytes 10616832 | tf_op jit(solution)/shard_map/all_gather | solution.py:49
  29.7 1508.4 %reduce-scatter.13.cloned.1.call-start = ((), (), s32[]{:S(2)}) async-start(), calls=%async_computation.15 | async-start | bytes 7077888 | tf_op jit(solution)/shard_map/reduce_scatter | solution.py:107
  30.1 327.6 %copy-start.1 = (f32[256,64]{0,1:T(8,128)}, f32[256,64]{0,1:T(8,128)S(1)}, u32[]{:S(2)}) copy-start(f32[256,64]{0,1:T(8,128)S(1)} %get-tuple-element.23) | copy-start | bytes 196612
  30.1 327.6 %copy-start.4 = (f32[256,64]{0,1:T(8,128)}, f32[256,64]{0,1:T(8,128)S(1)}, u32[]{:S(2)}) copy-start(f32[256,64]{0,1:T(8,128)S(1)} %get-tuple-element.21) | copy-start | bytes 196612
  30.1 327.6 %copy-start.6 = (f32[256,64]{0,1:T(8,128)}, f32[256,64]{0,1:T(8,128)S(1)}, u32[]{:S(2)}) copy-start(f32[256,64]{0,1:T(8,128)S(1)} %get-tuple-element.22) | copy-start | bytes 196612
  846.5 24.7 %copy-start.2 = (f32[256,64]{0,1:T(8,128)S(1)}, f32[256,64]{0,1:T(8,128)}, u32[]{:S(2)}) copy-start(f32[256,64]{0,1:T(8,128)} %copy-done.1) | copy-start | bytes 196612
  846.5 24.7 %copy-start.7 = (f32[256,64]{0,1:T(8,128)S(1)}, f32[256,64]{0,1:T(8,128)}, u32[]{:S(2)}) copy-start(f32[256,64]{0,1:T(8,128)} %copy-done.6) | copy-start | bytes 196612
  910.4 23.0 %copy-start = (f32[256,64]{1,0:T(8,128)S(1)}, f32[256,64]{1,0:T(8,128)}, u32[]{:S(2)}) copy-start(f32[256,64]{1,0:T(8,128)} %copy.69) | copy-start | bytes 196612
  910.4 23.0 %copy-start.9 = (f32[256,64]{1,0:T(8,128)S(1)}, f32[256,64]{1,0:T(8,128)}, u32[]{:S(2)}) copy-start(f32[256,64]{1,0:T(8,128)} %copy.71) | copy-start | bytes 196612
  933.4 10.6 copy-start.14
  979.8 72.1 %copy-start.8 = (f32[256,64]{1,0:T(8,128)S(1)}, f32[256,64]{1,0:T(8,128)}, u32[]{:S(2)}) copy-start(f32[256,64]{1,0:T(8,128)} %copy.87) | copy-start | bytes 196612
  1089.3 450.8 %reduce-scatter.15.cloned.1.call-start = ((), (), s32[]{:S(2)}) async-start(), calls=%async_computation.16 | async-start | bytes 7077888 | tf_op jit(solution)/shard_map/reduce_scatter | solution.py:108
  1136.3 405.7 %reduce-scatter.17.cloned.1.call-start = ((), (), s32[]{:S(2)}) async-start(), calls=%async_computation.17 | async-start | bytes 21233664 | tf_op jit(solution)/shard_map/reduce_scatter | solution.py:109
  1210.4 86.4 %copy-start.3 = (f32[256,64]{0,1:T(8,128)S(1)}, f32[256,64]{0,1:T(8,128)}, u32[]{:S(2)}) copy-start(f32[256,64]{0,1:T(8,128)} %copy-done.1) | copy-start | bytes 196612
  1210.4 86.4 %copy-start.5 = (f32[256,64]{0,1:T(8,128)S(1)}, f32[256,64]{0,1:T(8,128)}, u32[]{:S(2)}) copy-start(f32[256,64]{0,1:T(8,128)} %copy-done.4) | copy-start | bytes 196612
  1210.4 334.4 %reduce-scatter.11.cloned.1.call-start = ((), (), s32[]{:S(2)}) async-start(), calls=%async_computation.14 | async-start | bytes 21233664 | tf_op jit(solution)/shard_map/reduce_scatter | solution.py:106
  1361.9 1.9 copy-start.16
  1361.9 405.1 %reduce-scatter.9.cloned.1.call-start = ((), (), s32[]{:S(2)}) async-start(), calls=%async_computation.13 | async-start | bytes 37748736 | tf_op jit(solution)/shard_map/reduce_scatter | solution.py:99
  1489.9 558.3 %reduce-scatter.7.cloned.1.call-start = ((), (), s32[]{:S(2)}) async-start(), calls=%async_computation.11 | async-start | bytes 37748736 | tf_op jit(solution)/shard_map/reduce_scatter | solution.py:76
  1538.1 228.9 %copy-start.11 = (f32[16,128]{1,0:T(8,128)S(1)}, f32[16,128]{1,0:T(8,128)}, u32[]{:S(2)}) copy-start(f32[16,128]{1,0:T(8,128)} %copy-done.10) | copy-start | bytes 24580
  1538.1 228.9 %copy-start.13 = (f32[3072]{0:T(1024)S(1)}, f32[3072]{0:T(1024)}, u32[]{:S(2)}) copy-start(f32[3072]{0:T(1024)} %param.9) | copy-start | bytes 36868
Sparse Core Ops, SparseCore 0:
  9.8 31.2 all-gather.8
  43.2 293.6 all-gather.6
  338.7 28.4 all-gather.10
  368.9 56.7 all-gather.14
  427.1 293.6 all-gather.16
  722.4 54.9 all-gather.12
  1089.4 56.1 reduce-scatter.12
  1148.9 56.1 reduce-scatter.14
  1210.5 120.4 reduce-scatter.16
  1362.0 120.7 reduce-scatter.10
  1490.0 276.8 reduce-scatter.8
  1769.1 279.0 reduce-scatter.6
where the time goes:
time: 2090 us; the launch traced here: 2080 us
  waiting for transfers between devices  1080 us (52%)
  matrix products  718 us (34%)
  other arithmetic  123 us (6%)
  local copies, waits for them, and re-layouts  108 us (5%)
  blocking collectives  33.6 us (2%)
    all_gather x1, waiting for transfers between devices, shard_body(): lax.all_gather((x_f * inv_rms * rms_gain).astype(low_type), 'tp', axis=1,...  296 us
    all_gather x1, waiting for transfers between devices, shard_body(): dy_full = lax.all_gather(dy_loc, 'tp', axis=1, tiled=True)  295 us
    reduce_scatter x1, waiting for transfers between devices, shard_body(): out_loc = lax.psum_scatter(out_part, 'tp', scatter_dimension=1, tiled=True)  233 us
    reduce_scatter x1, waiting for transfers between devices, shard_body(): lax.psum_scatter(d_normed_part, 'tp', scatter_dimension=1, tiled=True)  219 us
    dot_general x1, matrix products, shard_body(): jnp.einsum('bcgqk,bkcd->bqcgd', d_scores_bf, keys_rot, preferred_element_...  86.3 us
    dot_general x1, matrix products, shard_body(): jnp.einsum('bcgqk,bqcgd->bkcd', d_scores_bf, queries, preferred_element_t...  72.1 us
    dot_general x1, matrix products, shard_body(): jnp.einsum('bsj,dj->bsd', d_queries, wq_full, preferred_element_type=acc_...  67.4 us
    dot_general x1, matrix products, shard_body(): jnp.einsum('bsd,bsj->dj', normed, d_queries, preferred_element_type=acc_t...  49 us
  transfers between devices with their start and end apart: 12, of which 7 were waited for; matrix products, arithmetic and copies ran while one was open for 30% of the time, Pallas kernels for 0%

commit v1 on v0

v1 whole, which is shorter than its diff:
```python
import functools

import jax
import jax.numpy as jnp
from jax import lax
from jax.experimental import pallas as pl
from jax.experimental.pallas import tpu as pltpu
from jax.sharding import PartitionSpec as P


HEAD_DIM = 128
NORM_EPS = 1e-5
ROPE_THETA = 5.0e5
INV_FREQ = tuple(ROPE_THETA ** (-2.0 * pair_idx / HEAD_DIM) for pair_idx in range(HEAD_DIM // 2))
SCALE = HEAD_DIM ** -0.5
GROUPS = 2
F32 = jnp.float32
BF16 = jnp.bfloat16

VMEM_LIMIT = 56 * 1024 * 1024


def cost(flops, moved):
    return pl.CostEstimate(flops=flops, bytes_accessed=moved, transcendentals=0)


def dot_nn(a, b):
    return lax.dot_general(a, b, (((1,), (0,)), ((), ())), preferred_element_type=F32)


def dot_nt(a, b):
    return lax.dot_general(a, b, (((1,), (1,)), ((), ())), preferred_element_type=F32)


def dot_tn(a, b):
    return lax.dot_general(a, b, (((0,), (0,)), ((), ())), preferred_element_type=F32)


def rope_tables(seq_len):
    positions = jnp.arange(seq_len, dtype=F32)
    angles = positions[:, None] * jnp.asarray(INV_FREQ, dtype=F32)[None, :]
    cos, sin = jnp.cos(angles), jnp.sin(angles)
    return jnp.concatenate([cos, cos], axis=1), jnp.concatenate([-sin, sin], axis=1)


def swap_halves(vals):
    return pltpu.roll(vals, HEAD_DIM // 2, 1)


def attend_kernel(per_kv, n_kv, n_half, second_ref, tab_ref, *refs):
    q_refs, kv_refs, do_refs, kvx_refs = (refs[i * n_half:(i + 1) * n_half] for i in range(4))
    mixed_ref, dq_ref, dkv_own_ref, dkv_prev_ref = refs[4 * n_half:]
    seq = tab_ref.shape[1]
    kw = n_kv * HEAD_DIM

    def rope(vals, tab):
        vals_f = vals.astype(F32)
        return (vals_f * tab_ref[tab] + swap_halves(vals_f) * tab_ref[tab + 1]).astype(BF16)

    def unrope(vals, tab):
        return vals * tab_ref[tab] - swap_halves(vals) * tab_ref[tab + 1]

    def unit(half, kv, cross):
        cols = slice(kv * HEAD_DIM, (kv + 1) * HEAD_DIM)
        vcols = slice(kw + kv * HEAD_DIM, kw + (kv + 1) * HEAD_DIM)
        heads = [slice((kv * per_kv + i) * HEAD_DIM, (kv * per_kv + i + 1) * HEAD_DIM) for i in range(per_kv)]
        q = jnp.concatenate([rope(q_refs[half][:, h], 0) for h in heads], axis=0)
        d_out = jnp.concatenate([do_refs[half][:, h] for h in heads], axis=0)
        keys = rope(kv_refs[half][:, cols], 0)
        vals = kv_refs[half][:, vcols]
        key_pos = lax.broadcasted_iota(jnp.int32, (seq, seq), 0)
        query_pos = lax.broadcasted_iota(jnp.int32, (seq, seq), 1)
        causal = jnp.concatenate([key_pos <= query_pos] * per_kv, axis=1)
        if cross:
            keys = jnp.concatenate([keys, rope(kvx_refs[half][:, cols], 2)], axis=0)
            vals = jnp.concatenate([vals, kvx_refs[half][:, vcols]], axis=0)
        scores = dot_nt(keys, q) * SCALE
        own = jnp.where(causal, scores[:seq], -1e30)
        scores = jnp.concatenate([own, scores[seq:]], axis=0) if cross else own
        top = jnp.max(scores, axis=0, keepdims=True)
        weights = jnp.exp(scores - top)
        prob = weights * (1.0 / jnp.sum(weights, axis=0, keepdims=True))
        prob_bf = prob.astype(BF16)
        d_prob = dot_nt(vals, d_out)
        d_sum = jnp.sum(prob * d_prob, axis=0, keepdims=True)
        d_scores = ((prob * (d_prob - d_sum)) * SCALE).astype(BF16)
        mixed = dot_tn(prob_bf, vals).astype(BF16)
        d_q = dot_tn(d_scores, keys)
        d_vals = dot_nn(prob_bf, d_out)
        d_keys = dot_nn(d_scores, q)
        for i, h in enumerate(heads):
            rows = slice(i * seq, (i + 1) * seq)
            mixed_ref[half, :, h] = mixed[rows]
            dq_ref[half, :, h] = unrope(d_q[rows], 0).astype(BF16)
        dkv_own_ref[half, :, cols] = unrope(d_keys[:seq], 0)
        dkv_own_ref[half, :, vcols] = d_vals[:seq]
        if cross:
            dkv_prev_ref[half, :, cols] = unrope(d_keys[seq:], 2).astype(BF16)
            dkv_prev_ref[half, :, vcols] = d_vals[seq:].astype(BF16)

    def run(cross):
        for half in range(n_half):
            for kv in range(n_kv):
                unit(half, kv, cross)

    @pl.when(second_ref[0] == 0)
    def _():
        run(False)
        dkv_prev_ref[...] = jnp.zeros_like(dkv_prev_ref)

    @pl.when(second_ref[0] != 0)
    def _():
        run(True)


def attend(seq, second, tables, q, kv, d_mixed, kv_prev):
    n_half = len(q)
    tokens, qw = q[0].shape
    kw = kv[0].shape[1] // 2
    q_spec = pl.BlockSpec((seq, qw), lambda s: (s, 0))
    kv_spec = pl.BlockSpec((seq, 2 * kw), lambda s: (s, 0))

    def both(width):
        return pl.BlockSpec((n_half, seq, width), lambda s: (0, s, 0))

    flops = 6 * 2 * tokens * 2 * seq * n_half * qw
    return pl.pallas_call(
        functools.partial(attend_kernel, qw // kw, kw // HEAD_DIM, n_half),
        grid=(tokens // seq,),
        in_specs=[pl.BlockSpec(memory_space=pltpu.SMEM), pl.BlockSpec(tables.shape, lambda s: (0, 0, 0))]
        + [q_spec] * n_half + [kv_spec] * n_half + [q_spec] * n_half + [kv_spec] * n_half,
        out_specs=[both(qw), both(qw), both(2 * kw), both(2 * kw)],
        out_shape=[jax.ShapeDtypeStruct((n_half, tokens, qw), BF16), jax.ShapeDtypeStruct((n_half, tokens, qw), BF16),
                   jax.ShapeDtypeStruct((n_half, tokens, 2 * kw), F32), jax.ShapeDtypeStruct((n_half, tokens, 2 * kw), BF16)],
        compiler_params=pltpu.CompilerParams(dimension_semantics=("arbitrary",), vmem_limit_bytes=VMEM_LIMIT),
        cost_estimate=cost(4 * flops, n_half * tokens * (8 * qw + 14 * kw)),
        name="attend",
    )(second, tables, *q, *kv, *d_mixed, *kv_prev)


def prepare_kernel(x_ref, dy_ref, gain_ref, h_ref, ht_ref, dyt_ref):
    x_f = x_ref[...].astype(F32)
    inv_rms = lax.rsqrt(jnp.mean(x_f * x_f, axis=-1, keepdims=True) + NORM_EPS)
    h = (x_f * inv_rms * gain_ref[...]).astype(BF16)
    h_ref[...] = h
    ht_ref[...] = h.T
    dyt_ref[...] = dy_ref[...].T


def prepare(x, dy, gain):
    tokens, dim = x.shape
    block = 128
    row_spec = pl.BlockSpec((block, dim), lambda s: (s, 0))
    col_spec = pl.BlockSpec((dim, block), lambda s: (0, s))
    return pl.pallas_call(
        prepare_kernel,
        grid=(tokens // block,),
        in_specs=[row_spec, row_spec, pl.BlockSpec((1, dim), lambda s: (0, 0))],
        out_specs=[row_spec, col_spec, col_spec],
        out_shape=[jax.ShapeDtypeStruct((tokens, dim), BF16)] + [jax.ShapeDtypeStruct((dim, tokens), BF16)] * 2,
        compiler_params=pltpu.CompilerParams(dimension_semantics=("arbitrary",), vmem_limit_bytes=VMEM_LIMIT),
        cost_estimate=cost(60 * tokens * dim, 10 * tokens * dim),
        name="prepare",
    )(x, dy, gain.reshape(1, dim))


def weight_grad_kernel(at_ref, b_ref, out_ref):
    out_ref[0] = dot_nn(at_ref[...], b_ref[0])


def weight_grad(at, b):
    dim, tokens = at.shape
    n_half, _, width = b.shape
    rows = min(1024, dim)
    return pl.pallas_call(
        weight_grad_kernel,
        grid=(n_half, dim // rows),
        in_specs=[pl.BlockSpec((rows, tokens), lambda z, m: (m, 0)), pl.BlockSpec((1, tokens, width), lambda z, m: (z, 0, 0))],
        out_specs=pl.BlockSpec((1, rows, width), lambda z, m: (z, m, 0)),
        out_shape=jax.ShapeDtypeStruct((n_half, dim, width), F32),
        compiler_params=pltpu.CompilerParams(dimension_semantics=("arbitrary", "arbitrary"), vmem_limit_bytes=VMEM_LIMIT),
        cost_estimate=cost(2 * n_half * tokens * dim * width, n_half * (4 * dim * width + 2 * tokens * (width + dim))),
        name="weight_grad",
    )(at, b)


def gather_sum_kernel(n_pairs, n_half, has_res, *refs):
    acts, weights, out_ref = refs[:n_pairs], refs[n_pairs:2 * n_pairs], refs[-1]
    total = None
    for act, weight in zip(acts, weights):
        for half in range(n_half):
            term = dot_nt(act[half], weight[half])
            total = term if total is None else total + term
    rounded = total.astype(BF16)
    if has_res:
        rounded = (refs[2 * n_pairs][...].astype(F32) + rounded.astype(F32)).astype(BF16)
    out_ref[...] = rounded


def project_back(acts, weights, res=None):
    n_half, tokens, _ = acts[0].shape
    dim = weights[0].shape[1]
    bm, bn = min(1024, tokens), 512
    widths = [a.shape[2] for a in acts]
    out_spec = pl.BlockSpec((bm, bn), lambda m, n: (m, n))
    return pl.pallas_call(
        functools.partial(gather_sum_kernel, len(acts), n_half, res is not None),
        grid=(tokens // bm, dim // bn),
        in_specs=[pl.BlockSpec((n_half, bm, w), lambda m, n: (0, m, 0)) for w in widths]
        + [pl.BlockSpec((n_half, bn, w), lambda m, n: (0, n, 0)) for w in widths] + ([] if res is None else [out_spec]),
        out_specs=out_spec,
        out_shape=jax.ShapeDtypeStruct((tokens, dim), BF16),
        compiler_params=pltpu.CompilerParams(dimension_semantics=("arbitrary", "arbitrary"), vmem_limit_bytes=VMEM_LIMIT),
        cost_estimate=cost(2 * tokens * dim * n_half * sum(widths), 2 * n_half * (tokens + 2 * dim) * sum(widths) + 4 * tokens * dim),
        name="project_back",
    )(*acts, *weights, *([] if res is None else [res]))


def input_grad_kernel(x_ref, dy_ref, dh_ref, gain_ref, dx_ref, dgain_ref):
    x_f = x_ref[...].astype(F32)
    d_h = dh_ref[...].astype(F32)
    inv_rms = lax.rsqrt(jnp.mean(x_f * x_f, axis=-1, keepdims=True) + NORM_EPS)
    grad_gain = d_h * gain_ref[...]
    mean_gx = jnp.mean(grad_gain * x_f, axis=-1, keepdims=True)
    dx_ref[...] = (dy_ref[...].astype(F32) + inv_rms * (grad_gain - x_f * inv_rms * inv_rms * mean_gx)).astype(BF16)

    @pl.when(pl.program_id(0) == 0)
    def _():
        dgain_ref[...] = jnp.zeros_like(dgain_ref)

    dgain_ref[...] += jnp.sum(d_h * x_f * inv_rms, axis=0, keepdims=True)


def input_grad(x, dy, d_h, gain):
    tokens, dim = x.shape
    block = 128
    row_spec = pl.BlockSpec((block, dim), lambda s: (s, 0))
    gain_spec = pl.BlockSpec((1, dim), lambda s: (0, 0))
    return pl.pallas_call(
        input_grad_kernel,
        grid=(tokens // block,),
        in_specs=[row_spec, row_spec, row_spec, gain_spec],
        out_specs=[row_spec, gain_spec],
        out_shape=[jax.ShapeDtypeStruct((tokens, dim), BF16), jax.ShapeDtypeStruct((1, dim), F32)],
        compiler_params=pltpu.CompilerParams(dimension_semantics=("arbitrary",), vmem_limit_bytes=VMEM_LIMIT),
        cost_estimate=cost(60 * tokens * dim, 8 * tokens * dim),
        name="input_grad",
    )(x, dy, d_h, gain.reshape(1, dim))


def flip_kernel(w_ref, *out_refs):
    width = w_ref.shape[0] // len(out_refs)
    for i, out_ref in enumerate(out_refs):
        out_ref[...] = w_ref[i * width:(i + 1) * width, :].T


def flip(w, parts):
    rows, cols = w.shape
    shape = jax.ShapeDtypeStruct((cols, rows // parts), BF16)
    return pl.pallas_call(flip_kernel, out_shape=[shape] * parts, cost_estimate=cost(10 * rows * cols, 4 * rows * cols), name="flip")(w)


def finish_kernel(n_parts, splits, *refs):
    parts, outs = refs[:n_parts], refs[n_parts:]
    for p, part in enumerate(parts):
        width = part.shape[1] // splits
        for i, out in enumerate(outs):
            out[:, p * width:(p + 1) * width] = part[:, i * width:(i + 1) * width].astype(BF16)


def finish(parts, splits):
    rows, width = parts[0].shape
    shape = jax.ShapeDtypeStruct((rows, len(parts) * width // splits), BF16)
    return pl.pallas_call(functools.partial(finish_kernel, len(parts), splits), out_shape=[shape] * splits, name="finish",
                          cost_estimate=cost(10 * rows * width, 6 * rows * width))(*parts)


def finish_flip_kernel(*refs):
    parts, out = refs[:-1], refs[-1]
    width = parts[0].shape[1]
    for p, part in enumerate(parts):
        out[p * width:(p + 1) * width, :] = part[...].T.astype(BF16)


def finish_flip(parts):
    rows, width = parts[0].shape
    shape = jax.ShapeDtypeStruct((len(parts) * width, rows), BF16)
    return pl.pallas_call(finish_flip_kernel, out_shape=shape, name="finish_flip",
                          cost_estimate=cost(10 * rows * width, 6 * rows * width))(*parts)


def after(dep, value):
    return lax.optimization_barrier((dep, value))[1]


def solution(mesh):
    tp = mesh.shape['tp']
    everyone = ('tp', 'fsdp')
    act_spec = P('fsdp', 'tp', None)
    col_spec = P('fsdp', 'tp')
    row_spec = P('tp', 'fsdp')

    def shard_body(x_loc, gain, wq_loc, wk_loc, wv_loc, wo_loc, dy_loc):
        batch, seq, dim = x_loc.shape
        tokens = batch * seq
        q_cols, kv_cols = wq_loc.shape[1], wk_loc.shape[1]
        tp_idx = lax.axis_index('tp')

        def gather(block):
            return lax.all_gather(block, everyone, axis=0, tiled=True).reshape(tp, dim, block.shape[1])

        def scatter(parts):
            return lax.psum_scatter(parts.reshape(tp * dim, parts.shape[2]), everyone, scatter_dimension=0, tiled=True)

        kw, qw = kv_cols // GROUPS, q_cols // GROUPS
        wo_flipped = flip(wo_loc, GROUPS)
        wkv, wq, wo = [], [], []
        for g in range(GROUPS):
            ks = slice(g * kw, (g + 1) * kw)
            wkv.append(gather(jnp.concatenate([wk_loc[:, ks], wv_loc[:, ks]], axis=1)))
            wq.append(gather(wq_loc[:, g * qw:(g + 1) * qw]))
            wo.append(gather(wo_flipped[g]))

        x = x_loc.reshape(tokens, dim)
        dy = dy_loc.reshape(tokens, dim)
        normed, normed_t, dy_t = prepare(x, dy, gain)

        cos_tab, sin_tab = rope_tables(seq * tp)
        tables = jnp.stack([lax.dynamic_slice_in_dim(cos_tab, tp_idx * seq, seq), lax.dynamic_slice_in_dim(sin_tab, tp_idx * seq, seq),
                            cos_tab[:seq], sin_tab[:seq]])
        second = tp_idx.astype(jnp.int32).reshape(1)

        def project(act, weights, dep):
            act = after(dep, act)
            return [dot_nn(act, weights[z]).astype(BF16) for z in range(tp)]

        def attend_group(kv_g, kv_prev_g, q_g, d_mixed, dep):
            return attend(seq, second, after(dep, tables), q_g, kv_g, d_mixed, kv_prev_g)

        def send_kv(kv_g):
            return [lax.ppermute(part, 'tp', [(0, 1)]) for part in kv_g]

        def kv_grad(own, prev):
            return (own + lax.ppermute(prev, 'tp', [(1, 0)]).astype(F32)).astype(BF16)

        assert GROUPS == 2
        kv0 = project(normed, wkv[0], normed)
        prev0 = send_kv(kv0)
        q0 = project(normed, wq[0], kv0[-1])
        d_mixed0 = project(dy, wo[0], q0[-1])
        kv1 = project(normed, wkv[1], d_mixed0[-1])
        prev1 = send_kv(kv1)
        mixed0, d_q0, own0, back0 = attend_group(kv0, prev0, q0, d_mixed0, kv1[-1])
        d_kv0 = kv_grad(own0, back0)
        part = weight_grad(after(mixed0, dy_t), mixed0)
        dwo0 = scatter(part)
        part = weight_grad(after(part, normed_t), d_q0)
        dwq0 = scatter(part)
        q1 = project(normed, wq[1], part)
        d_mixed1 = project(dy, wo[1], q1[-1])
        mixed1, d_q1, own1, back1 = attend_group(kv1, prev1, q1, d_mixed1, d_mixed1[-1])
        d_kv1 = kv_grad(own1, back1)
        part = weight_grad(after(mixed1, normed_t), d_kv0)
        dwkv0 = scatter(part)
        part = weight_grad(after(part, dy_t), mixed1)
        dwo1 = scatter(part)
        part = weight_grad(after(part, normed_t), d_q1)
        dwq1 = scatter(part)
        y = project_back([mixed0, mixed1], wo, after(part, x))
        part = weight_grad(after(y, normed_t), d_kv1)
        dwkv1 = scatter(part)
        d_normed = project_back([after(part, d_q0), d_q1, d_kv0, d_kv1], wq + wkv)
        dx, d_gain = input_grad(x, dy, d_normed, gain)
        d_gain = lax.psum(d_gain.reshape(dim), everyone)

        dwo_loc = finish_flip([dwo0, dwo1])
        dwq_loc, = finish([dwq0, dwq1], 1)
        dwk_loc, dwv_loc = finish([dwkv0, dwkv1], 2)
        return (y.reshape(x_loc.shape), dx.reshape(x_loc.shape), dwq_loc, dwk_loc, dwv_loc, dwo_loc, d_gain)

    return jax.shard_map(shard_body, mesh=mesh,
                         in_specs=(act_spec, P(), col_spec, col_spec, col_spec, row_spec, act_spec),
                         out_specs=(act_spec, act_spec, col_spec, col_spec, col_spec, row_spec, P()),
                         check_vma=False)
```

time: 2090 us -> 1300 us (0.62)
  matrix products: 718 us -> 162 us
  waiting for transfers between devices: 1080 us -> 635 us
  Pallas kernels: 0 us -> 412 us
  other arithmetic: 123 us -> 17.8 us
  local copies, waits for them, and re-layouts: 108 us -> 3.65 us
    dot_general x17 -> x12, matrix products: 682 us -> 162 us  [dot_nn(): lax.dot_general(a, b, (((1,), (0,)), ((), ())), preferred_element_type=F32)]
    all_gather x6, waiting for transfers between devices: 629 us -> 158 us  [gather(): lax.all_gather(block, everyone, axis=0, tiled=True)]
    pallas_call x0 -> x16, Pallas kernels: none -> 412 us  [the longest x6 147 us: weight_grad(): pl.pallas_call(weight_grad_kernel, grid=(n_half, dim // rows), in_specs=[...]
    convert_element_type x3 -> x0, local copies, waits for them, and re-layouts: 51.5 us -> none  [the longest x2 34.9 us: rotate(): vals_f = head_vals.astype(jnp.float32)]
    ppermute x0 -> x6, waiting for transfers between devices: none -> 47.9 us  [the longest x2 47.8 us: kv_grad(): return (own + lax.ppermute(prev, 'tp', [(1, 0)]).astype(F32)).astype(BF16)]
    another operation x4 -> x2, other arithmetic: 43.8 us -> 0.86 us  [shard_body(): jnp.stack([lax.dynamic_slice_in_dim(cos_tab, tp_idx * seq, seq), lax.dyna...]
    sub x1 -> x0, matrix products: 35.9 us -> none  [shard_body(): attn_prob = jax.nn.softmax(jnp.where(causal, scores, -1e+30), axis=-1)]
    convert_element_type x6 -> x2, other arithmetic: 47.8 us -> 14.9 us  [kv_grad(): return (own + lax.ppermute(prev, 'tp', [(1, 0)]).astype(F32)).astype(BF16)]
  transfers between devices with their start and end apart: 12 -> 18, of which waited for: 7 -> 9; matrix products, arithmetic and copies ran while one was open for 30% -> 13% of each run, Pallas kernels for 0% -> 30%
where the time goes in v1:
time: 1300 us
  waiting for transfers between devices  635 us (49%)
  Pallas kernels  412 us (32%)
  matrix products  162 us (12%)
  blocking collectives  32.3 us (2%)
  starting transfers between devices  18.7 us (1%)
  other arithmetic  17.8 us (1%)
  between operations  14.6 us (1%)
    reduce_scatter x6, waiting for transfers between devices, scatter(): lax.psum_scatter(parts.reshape(tp * dim, parts.shape[2]), everyone, scatt...  426 us
    dot_general x12, matrix products, dot_nn(): lax.dot_general(a, b, (((1,), (0,)), ((), ())), preferred_element_type=F32)  162 us
    all_gather x6, waiting for transfers between devices, gather(): lax.all_gather(block, everyone, axis=0, tiled=True)  158 us
    pallas_call x6, Pallas kernels, weight_grad(): pl.pallas_call(weight_grad_kernel, grid=(n_half, dim // rows), in_specs=[...  147 us
    pallas_call x2, Pallas kernels, project_back(): pl.pallas_call(functools.partial(gather_sum_kernel, len(acts), n_half, re...  126 us
    pallas_call x2, Pallas kernels, attend(): pl.pallas_call(functools.partial(attend_kernel, qw // kw, kw // HEAD_DIM,...  71.4 us
    ppermute x2, waiting for transfers between devices, kv_grad(): return (own + lax.ppermute(prev, 'tp', [(1, 0)]).astype(F32)).astype(BF16)  47.8 us
    psum x1, blocking collectives, shard_body(): d_gain = lax.psum(d_gain.reshape(dim), everyone)  32.3 us
  transfers between devices with their start and end apart: 18, of which 9 were waited for; matrix products, arithmetic and copies ran while one was open for 13% of the time, Pallas kernels for 30%

profile of v1, /device:TPU:0, one launch (start us, length us, event | category | flops | bytes accessed | tf_op | source)
XLA Modules:
  0.0 1296.3 jit_solution(6362851219900419150)
XLA Ops:
  16.9 27.7 %prepare.1 = (bf16[2048,3072]{1,0:T(8,128)(2,1)}, bf16[3072,2048]{1,0:T(8,128)(2,1)}, bf16[3072,2048]{1,0:T(8,128)(2,1)}) custom-call(bf16[2048,3072]{1,0:T(8,128)(2,1)} %bitcast.39, bf16[2048,3072]{1,0:T(8,128)(2,1)} %bitcast.42, f32[1,3072]{1,0:T(1,128)} %bitcast.56), custom_call_target="tpu_custom_call" | custom-call | flops 377487360 | bytes 62914560 | tf_op jit(solution)/shard_map/prepare/pallas_call | solution.py:155
  55.8 11.7 fusion.48.refs_3_
  85.5 46.7 %all-gather.9.cloned.1.call-done = bf16[6144,768]{1,0:T(8,128)(2,1)} async-done(((bf16[384,768]{1,0:T(8,128)(2,1)}), bf16[6144,768]{1,0:T(8,128)(2,1)}) %all-gather.9.cloned.1.call-update) | async-done | bytes 9437200 | tf_op jit(solution)/shard_map/all_gather | solution.py:310
  132.2 15.4 %fusion.16.refs_1_ = bf16[2048,768]{1,0:T(8,128)(2,1)} fusion(bf16[2048,3072]{1,0:T(8,128)(2,1)} %get-tuple-element.53, bf16[6144,768]{1,0:T(8,128)(2,1)} %all-gather.9.cloned.1.call-done), kind=kOutput, calls=%fused_computation.18 | convolution fusion | flops 9665249280 | bytes 20447232 | tf_op jit(solution)/shard_map/dot_general | solution.py:28
  147.6 68.3 %all-gather.11.cloned.1.call-done = bf16[6144,768]{1,0:T(8,128)(2,1)} async-done(((bf16[384,768]{1,0:T(8,128)(2,1)}), bf16[6144,768]{1,0:T(8,128)(2,1)}) %all-gather.11.cloned.1.call-update) | async-done | bytes 9437200 | tf_op jit(solution)/shard_map/all_gather | solution.py:310
  216.0 15.4 %fusion.19.refs_5_ = bf16[2048,768]{1,0:T(8,128)(2,1)} fusion(bf16[2048,3072]{1,0:T(8,128)(2,1)} %bitcast.43, bf16[6144,768]{1,0:T(8,128)(2,1)} %all-gather.11.cloned.1.call-done), kind=kOutput, calls=%fused_computation.19 | convolution fusion | flops 9665249280 | bytes 20447232 | tf_op jit(solution)/shard_map/dot_general | solution.py:28
  231.3 32.6 %all-gather.13.cloned.1.call-done = bf16[6144,512]{1,0:T(8,128)(2,1)} async-done(((bf16[384,512]{1,0:T(8,128)(2,1)}), bf16[6144,512]{1,0:T(8,128)(2,1)}) %all-gather.13.cloned.1.call-update) | async-done | bytes 6291472 | tf_op jit(solution)/shard_map/all_gather | solution.py:310
  264.0 11.7 fusion.51.refs_3_
  280.5 11.9 fusion.57.refs_2_
  295.5 12.9 fusion.25.refs_4_
  308.4 12.8 fusion.22.refs_0_
  321.2 35.7 %attend.2 = (bf16[2,2048,768]{2,1,0:T(8,128)(2,1)}, bf16[2,2048,768]{2,1,0:T(8,128)(2,1)}, f32[2,2048,512]{2,1,0:T(8,128)}, bf16[2,2048,512]{2,1,0:T(8,128)(2,1)}) custom-call(s32[1]{0:T(128)} %bitcast.second_ref, f32[4,128,128]{2,1,0:T(8,128)} %pad_maximum_fusion.2.tab_ref, bf16[2048,768]{1,0:T(8,128)(2,1)} %fusion.22.refs_0_, ...), custom_call_target="tpu_custom_call" | custom-call | flops 38654705664 | bytes 39845888 | tf_op jit(solution)/shard_map/attend/pallas_call | solution.py:127
  358.4 26.2 %weight_grad.6 = f32[2,3072,768]{2,1,0:T(8,128)} custom-call(bf16[3072,2048]{1,0:T(8,128)(2,1)} %get-tuple-element.61.at_ref, bf16[2,2048,768]{2,1,0:T(8,128)(2,1)} %get-tuple-element.47.b_ref.refs_0_), custom_call_target="tpu_custom_call" | custom-call | flops 19327352832 | bytes 50331648 | tf_op jit(solution)/shard_map/weight_grad/pallas_call | solution.py:175
  384.6 26.4 %weight_grad.7 = f32[2,3072,768]{2,1,0:T(8,128)} custom-call(bf16[3072,2048]{1,0:T(8,128)(2,1)} %get-tuple-element.65.at_ref, bf16[2,2048,768]{2,1,0:T(8,128)(2,1)} %get-tuple-element.68.b_ref.refs_0_), custom_call_target="tpu_custom_call" | custom-call | flops 19327352832 | bytes 50331648 | tf_op jit(solution)/shard_map/weight_grad/pallas_call | solution.py:175
  411.0 15.5 %fusion.28.refs_1_ = bf16[2048,768]{1,0:T(8,128)(2,1)} fusion(bf16[2048,3072]{1,0:T(8,128)(2,1)} %get-tuple-element.53, bf16[6144,768]{1,0:T(8,128)(2,1)} %all-gather.15.cloned.1.call-done), kind=kOutput, calls=%fused_computation.22 | convolution fusion | flops 9665249280 | bytes 20447232 | tf_op jit(solution)/shard_map/dot_general | solution.py:28
  426.5 14.2 %fusion.34.refs_0_ = bf16[2048,768]{1,0:T(8,128)(2,1)} fusion(bf16[2048,3072]{1,0:T(8,128)(2,1)} %get-tuple-element.53, bf16[6144,768]{1,0:T(8,128)(2,1)S(1)} %copy-done.1), kind=kOutput, calls=%fused_computation.24 | convolution fusion | flops 9665249280 | bytes 20447232 | tf_op jit(solution)/shard_map/dot_general | solution.py:28
  440.7 16.0 %fusion.31.refs_5_ = bf16[2048,768]{1,0:T(8,128)(2,1)} fusion(bf16[2048,3072]{1,0:T(8,128)(2,1)} %bitcast.44, bf16[6144,768]{1,0:T(8,128)(2,1)} %all-gather.17.cloned.1.call-done), kind=kOutput, calls=%fused_computation.23 | convolution fusion | flops 9665249280 | bytes 20447232 | tf_op jit(solution)/shard_map/dot_general | solution.py:28
  456.6 14.0 %fusion.37.refs_4_ = bf16[2048,768]{1,0:T(8,128)(2,1)} fusion(bf16[2048,3072]{1,0:T(8,128)(2,1)} %bitcast.45, bf16[6144,768]{1,0:T(8,128)(2,1)S(1)} %copy-done.2), kind=kOutput, calls=%fused_computation.25 | convolution fusion | flops 9665249280 | bytes 20447232 | tf_op jit(solution)/shard_map/dot_general | solution.py:28
  470.6 35.7 %attend.3 = (bf16[2,2048,768]{2,1,0:T(8,128)(2,1)}, bf16[2,2048,768]{2,1,0:T(8,128)(2,1)}, f32[2,2048,512]{2,1,0:T(8,128)}, bf16[2,2048,512]{2,1,0:T(8,128)(2,1)}) custom-call(s32[1]{0:T(128)} %bitcast.second_ref, f32[4,128,128]{2,1,0:T(8,128)} %pad_maximum_fusion.2.tab_ref, bf16[2048,768]{1,0:T(8,128)(2,1)} %fusion.34.refs_0_, ...), custom_call_target="tpu_custom_call" | custom-call | flops 38654705664 | bytes 39845888 | tf_op jit(solution)/shard_map/attend/pallas_call | solution.py:127
  514.3 20.2 %weight_grad.8 = f32[2,3072,512]{2,1,0:T(8,128)} custom-call(bf16[3072,2048]{1,0:T(8,128)(2,1)} %get-tuple-element.65.at_ref, bf16[2,2048,512]{2,1,0:T(8,128)(2,1)} %add_convert_fusion.1.b_ref.refs_2_), custom_call_target="tpu_custom_call" | custom-call | flops 12884901888 | bytes 41943040 | tf_op jit(solution)/shard_map/weight_grad/pallas_call | solution.py:175
  535.9 26.3 %weight_grad.9 = f32[2,3072,768]{2,1,0:T(8,128)} custom-call(bf16[3072,2048]{1,0:T(8,128)(2,1)} %get-tuple-element.61.at_ref, bf16[2,2048,768]{2,1,0:T(8,128)(2,1)} %get-tuple-element.57.b_ref.refs_1_), custom_call_target="tpu_custom_call" | custom-call | flops 19327352832 | bytes 50331648 | tf_op jit(solution)/shard_map/weight_grad/pallas_call | solution.py:175
  562.2 28.3 %weight_grad.10 = f32[2,3072,768]{2,1,0:T(8,128)} custom-call(bf16[3072,2048]{1,0:T(8,128)(2,1)} %get-tuple-element.65.at_ref, bf16[2,2048,768]{2,1,0:T(8,128)(2,1)} %get-tuple-element.63.b_ref.refs_1_), custom_call_target="tpu_custom_call" | custom-call | flops 19327352832 | bytes 50331648 | tf_op jit(solution)/shard_map/weight_grad/pallas_call | solution.py:175
  590.4 48.6 %project_back.2 = bf16[2048,3072]{1,0:T(8,128)(2,1)} custom-call(bf16[2,2048,768]{2,1,0:T(8,128)(2,1)} %get-tuple-element.47.b_ref.refs_0_, bf16[2,2048,768]{2,1,0:T(8,128)(2,1)} %get-tuple-element.57.b_ref.refs_1_, bf16[2,3072,768]{2,1,0:T(8,128)(2,1)} %bitcast.64, bf16[2,3072,768]{2,1,0:T(8,128)(2,1)} %bitcast.65, bf16[2048,3072]{1,0:T(8,128)(2,1)} %bitcast.40), custom_call_target="tpu_custom_call" | custom-call | flops 38654705664 | bytes 75497472 | tf_op jit(solution)/shard_map/project_back/pallas_call | solution.py:206
  639.0 47.8 %collective-permute-done.5 = bf16[2,2048,512]{2,1,0:T(8,128)(2,1)S(1)} collective-permute-done((bf16[2,2048,512]{2,1,0:T(8,128)(2,1)}, bf16[2,2048,512]{2,1,0:T(8,128)(2,1)S(1)}, u32[]{:S(2)}, u32[]{:S(2)}) %collective-permute-start.5) | collective-permute-done | bytes 4194336 | tf_op jit(solution)/shard_map/ppermute | solution.py:344
  693.8 20.2 %weight_grad.11 = f32[2,3072,512]{2,1,0:T(8,128)} custom-call(bf16[3072,2048]{1,0:T(8,128)(2,1)} %get-tuple-element.65.at_ref, bf16[2,2048,512]{2,1,0:T(8,128)(2,1)} %add_convert_fusion.b_ref.refs_3_), custom_call_target="tpu_custom_call" | custom-call | flops 12884901888 | bytes 41943040 | tf_op jit(solution)/shard_map/weight_grad/pallas_call | solution.py:175
  716.6 77.4 %project_back.3.dh_ref = bf16[2048,3072]{1,0:T(8,128)(2,1)} custom-call(bf16[2,2048,768]{2,1,0:T(8,128)(2,1)} %get-tuple-element.68.b_ref.refs_0_, bf16[2,2048,768]{2,1,0:T(8,128)(2,1)} %get-tuple-element.63.b_ref.refs_1_, bf16[2,2048,512]{2,1,0:T(8,128)(2,1)} %add_convert_fusion.1.b_ref.refs_2_, bf16[2,2048,512]{2,1,0:T(8,128)(2,1)} %add_convert_fusion.b_ref.refs_3_, ...), custom_call_target="tpu_custom_call" | custom-call | flops 64424509440 | bytes 109051904 | tf_op jit(solution)/shard_map/project_back/pallas_call | solution.py:206
  794.0 29.0 %input_grad.1 = (bf16[2048,3072]{1,0:T(8,128)(2,1)}, f32[1,3072]{1,0:T(1,128)}) custom-call(bf16[2048,3072]{1,0:T(8,128)(2,1)} %bitcast.41, bf16[2048,3072]{1,0:T(8,128)(2,1)} %bitcast.46, bf16[2048,3072]{1,0:T(8,128)(2,1)} %project_back.3.dh_ref, f32[1,3072]{1,0:T(1,128)} %bitcast.57), custom_call_target="tpu_custom_call" | custom-call | flops 377487360 | bytes 50331648 | tf_op jit(solution)/shard_map/input_grad/pallas_call | solution.py:239
  822.9 32.3 %psum.7 = f32[3072]{0:T(1024)} all-reduce(f32[3072]{0:T(1024)} %bitcast.58), channel_id=1, replica_groups=mesh['tp'=2,'fsdp'=8] {'tp','fsdp'}, use_global_device_ids=true, to_apply=%region_6.0 | all-reduce | flops 3072 | bytes 24576 | tf_op jit(solution)/shard_map/psum | solution.py:374
  857.6 68.4 %reduce-scatter.15.cloned.1.call-done.refs_0_ = f32[384,768]{1,0:T(8,128)} async-done(((f32[6144,768]{1,0:T(8,128)}), f32[384,768]{1,0:T(8,128)}) %reduce-scatter.15.cloned.1.call-update) | async-done | bytes 1179664 | tf_op jit(solution)/shard_map/reduce_scatter | solution.py:313
  926.0 120.1 %reduce-scatter.17.cloned.1.call-done.refs_1_ = f32[384,768]{1,0:T(8,128)} async-done(((f32[6144,768]{1,0:T(8,128)}), f32[384,768]{1,0:T(8,128)}) %reduce-scatter.17.cloned.1.call-update) | async-done | bytes 1179664 | tf_op jit(solution)/shard_map/reduce_scatter | solution.py:313
  1049.1 117.2 %reduce-scatter.7.cloned.1.call-done.refs_0_ = f32[384,768]{1,0:T(8,128)} async-done(((f32[6144,768]{1,0:T(8,128)}), f32[384,768]{1,0:T(8,128)}) %reduce-scatter.7.cloned.1.call-update) | async-done | bytes 1179664 | tf_op jit(solution)/shard_map/reduce_scatter | solution.py:313
  1166.3 120.1 %reduce-scatter.9.cloned.1.call-done.refs_1_ = f32[384,768]{1,0:T(8,128)} async-done(((f32[6144,768]{1,0:T(8,128)}), f32[384,768]{1,0:T(8,128)}) %reduce-scatter.9.cloned.1.call-update) | async-done | bytes 1179664 | tf_op jit(solution)/shard_map/reduce_scatter | solution.py:313
  (78 shorter events, 75.3 us)
Async XLA Ops:
  7.2 9.2 copy-start
  7.2 48.6 %all-gather.7.cloned.1.call-start = ((), (), s32[]{:S(2)}) async-start(), calls=%async_computation.6 | async-start | bytes 6684672 | tf_op jit(solution)/shard_map/all_gather | solution.py:310
  9.3 122.9 %all-gather.9.cloned.1.call-start = ((), (), s32[]{:S(2)}) async-start(), calls=%async_computation.7 | async-start | bytes 10027008 | tf_op jit(solution)/shard_map/all_gather | solution.py:310
  11.7 204.3 %all-gather.11.cloned.1.call-start = ((), (), s32[]{:S(2)}) async-start(), calls=%async_computation.8 | async-start | bytes 10027008 | tf_op jit(solution)/shard_map/all_gather | solution.py:310
  14.3 249.7 %all-gather.13.cloned.1.call-start = ((), (), s32[]{:S(2)}) async-start(), calls=%async_computation.9 | async-start | bytes 6684672 | tf_op jit(solution)/shard_map/all_gather | solution.py:310
  15.2 395.8 %all-gather.15.cloned.1.call-start = ((), (), s32[]{:S(2)}) async-start(), calls=%async_computation.10 | async-start | bytes 10027008 | tf_op jit(solution)/shard_map/all_gather | solution.py:310
  15.7 424.9 %all-gather.17.cloned.1.call-start = ((), (), s32[]{:S(2)}) async-start(), calls=%async_computation.11 | async-start | bytes 10027008 | tf_op jit(solution)/shard_map/all_gather | solution.py:310
  16.3 838.9 %reduce-scatter.11.cloned.1.call-start = ((), (), s32[]{:S(2)}) async-start(), calls=%async_computation.14 | async-start | bytes 13369344 | tf_op jit(solution)/shard_map/reduce_scatter | solution.py:313
  55.8 16.2 %copy-start.3 = (bf16[6144,512]{1,0:T(8,128)(2,1)S(1)}, bf16[6144,512]{1,0:T(8,128)(2,1)}, u32[]{:S(2)}) copy-start(bf16[6144,512]{1,0:T(8,128)(2,1)} %all-gather.7.cloned.1.call-done) | copy-start | bytes 18874372
  67.4 253.8 %collective-permute-start.1 = (bf16[2048,512]{1,0:T(8,128)(2,1)}, bf16[2048,512]{1,0:T(8,128)(2,1)}, u32[]{:S(2)}, u32[]{:S(2)}) collective-permute-start(bf16[2048,512]{1,0:T(8,128)(2,1)} %fusion.48.refs_3_), channel_id=1, source_target_pairs={{0,8},{1,9},{2,10},{3,11},{4,12},{5,13},{6,14},{7,15}} | collective-permute-start | bytes 6291464 | tf_op jit(solution)/shard_map/ppermute | solution.py:341
  82.5 238.7 %collective-permute-start = (bf16[2048,512]{1,0:T(8,128)(2,1)}, bf16[2048,512]{1,0:T(8,128)(2,1)}, u32[]{:S(2)}, u32[]{:S(2)}) collective-permute-start(bf16[2048,512]{1,0:T(8,128)(2,1)} %fusion.54.refs_2_), channel_id=1, source_target_pairs={{0,8},{1,9},{2,10},{3,11},{4,12},{5,13},{6,14},{7,15}} | collective-permute-start | bytes 6291464 | tf_op jit(solution)/shard_map/ppermute | solution.py:341
  264.0 16.5 %copy-start.4 = (bf16[6144,512]{1,0:T(8,128)(2,1)S(1)}, bf16[6144,512]{1,0:T(8,128)(2,1)}, u32[]{:S(2)}) copy-start(bf16[6144,512]{1,0:T(8,128)(2,1)} %all-gather.13.cloned.1.call-done) | copy-start | bytes 18874372
  264.0 31.4 %slice-start = ((s8[12582912]{0:T(1024)(128)(4,1)}), s8[4194304]{0:T(1024)(128)(4,1)S(1)}, s32[]{:S(2)}) async-start(s8[12582912]{0:T(1024)(128)(4,1)} %bitcast.47), calls=%async_computation.18 | async-start | bytes 8388608
  264.0 31.5 %slice-start.1 = ((s8[12582912]{0:T(1024)(128)(4,1)}), s8[4194304]{0:T(1024)(128)(4,1)S(1)}, s32[]{:S(2)}) async-start(s8[12582912]{0:T(1024)(128)(4,1)} %bitcast.47), calls=%async_computation.19 | async-start | bytes 8388608
  275.6 19.8 %slice-start.2 = ((s8[12582912]{0:T(1024)(128)(4,1)}), s8[4194304]{0:T(1024)(128)(4,1)S(1)}, s32[]{:S(2)}) async-start(s8[12582912]{0:T(1024)(128)(4,1)} %bitcast.47), calls=%async_computation.20 | async-start | bytes 8388608
  275.6 195.0 %collective-permute-start.3 = (bf16[2048,512]{1,0:T(8,128)(2,1)}, bf16[2048,512]{1,0:T(8,128)(2,1)}, u32[]{:S(2)}, u32[]{:S(2)}) collective-permute-start(bf16[2048,512]{1,0:T(8,128)(2,1)} %fusion.51.refs_3_), channel_id=1, source_target_pairs={{0,8},{1,9},{2,10},{3,11},{4,12},{5,13},{6,14},{7,15}} | collective-permute-start | bytes 6291464 | tf_op jit(solution)/shard_map/ppermute | solution.py:341
  280.5 27.9 %slice-start.3 = ((s8[12582912]{0:T(1024)(128)(4,1)}), s8[4194304]{0:T(1024)(128)(4,1)S(1)}, s32[]{:S(2)}) async-start(s8[12582912]{0:T(1024)(128)(4,1)} %bitcast.59), calls=%async_computation.21 | async-start | bytes 8388608
  280.5 27.9 %slice-start.4 = ((s8[12582912]{0:T(1024)(128)(4,1)}), s8[4194304]{0:T(1024)(128)(4,1)S(1)}, s32[]{:S(2)}) async-start(s8[12582912]{0:T(1024)(128)(4,1)} %bitcast.59), calls=%async_computation.22 | async-start | bytes 8388608
  292.3 16.0 %slice-start.5 = ((s8[12582912]{0:T(1024)(128)(4,1)}), s8[4194304]{0:T(1024)(128)(4,1)S(1)}, s32[]{:S(2)}) async-start(s8[12582912]{0:T(1024)(128)(4,1)} %bitcast.59), calls=%async_computation.23 | async-start | bytes 8388608
  292.3 178.3 %collective-permute-start.2 = (bf16[2048,512]{1,0:T(8,128)(2,1)}, bf16[2048,512]{1,0:T(8,128)(2,1)}, u32[]{:S(2)}, u32[]{:S(2)}) collective-permute-start(bf16[2048,512]{1,0:T(8,128)(2,1)} %fusion.57.refs_2_), channel_id=1, source_target_pairs={{0,8},{1,9},{2,10},{3,11},{4,12},{5,13},{6,14},{7,15}} | collective-permute-start | bytes 6291464 | tf_op jit(solution)/shard_map/ppermute | solution.py:341
  356.9 149.5 %collective-permute-start.4 = (bf16[2,2048,512]{2,1,0:T(8,128)(2,1)}, bf16[2,2048,512]{2,1,0:T(8,128)(2,1)}, u32[]{:S(2)}, u32[]{:S(2)}) collective-permute-start(bf16[2,2048,512]{2,1,0:T(8,128)(2,1)} %get-tuple-element.60), channel_id=1, source_target_pairs={{8,0},{9,1},{10,2},{11,3},{12,4},{13,5},{14,6},{15,7}} | collective-permute-start | bytes 12582920 | tf_op jit(solution)/shard_map/ppermute | solution.py:344
  411.0 15.5 %copy-start.1 = (bf16[6144,768]{1,0:T(8,128)(2,1)S(1)}, bf16[6144,768]{1,0:T(8,128)(2,1)}, u32[]{:S(2)}) copy-start(bf16[6144,768]{1,0:T(8,128)(2,1)} %all-gather.15.cloned.1.call-done) | copy-start | bytes 28311556
  440.7 16.0 %copy-start.2 = (bf16[6144,768]{1,0:T(8,128)(2,1)S(1)}, bf16[6144,768]{1,0:T(8,128)(2,1)}, u32[]{:S(2)}) copy-start(bf16[6144,768]{1,0:T(8,128)(2,1)} %all-gather.17.cloned.1.call-done) | copy-start | bytes 28311556
  534.5 320.8 %reduce-scatter.13.cloned.1.call-start = ((), (), s32[]{:S(2)}) async-start(), calls=%async_computation.15 | async-start | bytes 13369344 | tf_op jit(solution)/shard_map/reduce_scatter | solution.py:313
  534.6 152.3 %collective-permute-start.5 = (bf16[2,2048,512]{2,1,0:T(8,128)(2,1)}, bf16[2,2048,512]{2,1,0:T(8,128)(2,1)S(1)}, u32[]{:S(2)}, u32[]{:S(2)}) collective-permute-start(bf16[2,2048,512]{2,1,0:T(8,128)(2,1)} %get-tuple-element.67), channel_id=1, source_target_pairs={{8,0},{9,1},{10,2},{11,3},{12,4},{13,5},{14,6},{15,7}} | collective-permute-start | bytes 12582920 | tf_op jit(solution)/shard_map/ppermute | solution.py:344
  713.9 212.0 %reduce-scatter.15.cloned.1.call-start = ((), (), s32[]{:S(2)}) async-start(), calls=%async_computation.16 | async-start | bytes 20054016 | tf_op jit(solution)/shard_map/reduce_scatter | solution.py:313
  714.7 331.4 %reduce-scatter.17.cloned.1.call-start = ((), (), s32[]{:S(2)}) async-start(), calls=%async_computation.17 | async-start | bytes 20054016 | tf_op jit(solution)/shard_map/reduce_scatter | solution.py:313
  715.3 451.1 %reduce-scatter.7.cloned.1.call-start = ((), (), s32[]{:S(2)}) async-start(), calls=%async_computation.12 | async-start | bytes 20054016 | tf_op jit(solution)/shard_map/reduce_scatter | solution.py:313
  716.0 570.5 %reduce-scatter.9.cloned.1.call-start = ((), (), s32[]{:S(2)}) async-start(), calls=%async_computation.13 | async-start | bytes 20054016 | tf_op jit(solution)/shard_map/reduce_scatter | solution.py:313
Sparse Core Ops, SparseCore 0:
  10.8 44.9 all-gather.6
  58.6 73.6 all-gather.8
  134.5 81.4 all-gather.10
  218.6 45.3 all-gather.12
  266.6 73.6 all-gather.14
  342.4 86.3 all-gather.16
  534.6 150.5 reduce-scatter.10
  714.1 91.1 reduce-scatter.12
  810.1 115.8 reduce-scatter.14
  930.7 115.3 reduce-scatter.16
  1051.0 115.3 reduce-scatter.6
  1171.1 115.3 reduce-scatter.8

commit v2 on v1

--- a/solution.py
+++ b/solution.py
@@ -5,6 +5,7 @@
 from jax import lax
 from jax.experimental import pallas as pl
 from jax.experimental.pallas import tpu as pltpu
+from jax.sharding import Mesh
 from jax.sharding import PartitionSpec as P
 
 
@@ -13,7 +14,7 @@
 ROPE_THETA = 5.0e5
 INV_FREQ = tuple(ROPE_THETA ** (-2.0 * pair_idx / HEAD_DIM) for pair_idx in range(HEAD_DIM // 2))
 SCALE = HEAD_DIM ** -0.5
-GROUPS = 2
+CORES = 2
 F32 = jnp.float32
 BF16 = jnp.bfloat16
 
@@ -164,56 +165,65 @@
     )(x, dy, gain.reshape(1, dim))
 
 
-def weight_grad_kernel(at_ref, b_ref, out_ref):
-    out_ref[0] = dot_nn(at_ref[...], b_ref[0])
+def weight_grad_kernel(n_sets, *refs):
+    total = None
+    for at_ref, b_ref in zip(refs[:n_sets], refs[n_sets:2 * n_sets]):
+        term = dot_nn(at_ref[...], b_ref[0])
+        total = term if total is None else total + term
+    refs[-1][0] = total
 
 
 def weight_grad(at, b):
-    dim, tokens = at.shape
-    n_half, _, width = b.shape
+    dim, tokens = at[0].shape
+    n_half, _, width = b[0].shape
+    n_sets = len(at)
     rows = min(1024, dim)
     return pl.pallas_call(
-        weight_grad_kernel,
+        functools.partial(weight_grad_kernel, n_sets),
         grid=(n_half, dim // rows),
-        in_specs=[pl.BlockSpec((rows, tokens), lambda z, m: (m, 0)), pl.BlockSpec((1, tokens, width), lambda z, m: (z, 0, 0))],
+        in_specs=[pl.BlockSpec((rows, tokens), lambda z, m: (m, 0))] * n_sets
+        + [pl.BlockSpec((1, tokens, width), lambda z, m: (z, 0, 0))] * n_sets,
         out_specs=pl.BlockSpec((1, rows, width), lambda z, m: (z, m, 0)),
         out_shape=jax.ShapeDtypeStruct((n_half, dim, width), F32),
         compiler_params=pltpu.CompilerParams(dimension_semantics=("arbitrary", "arbitrary"), vmem_limit_bytes=VMEM_LIMIT),
-        cost_estimate=cost(2 * n_half * tokens * dim * width, n_half * (4 * dim * width + 2 * tokens * (width + dim))),
+        cost_estimate=cost(2 * n_sets * n_half * tokens * dim * width, n_half * (4 * dim * width + 2 * n_sets * tokens * (width + dim))),
         name="weight_grad",
-    )(at, b)
-
-
-def gather_sum_kernel(n_pairs, n_half, has_res, *refs):
-    acts, weights, out_ref = refs[:n_pairs], refs[n_pairs:2 * n_pairs], refs[-1]
+    )(*at, *b)
+
+
+def project_back_kernel(n_pairs, n_half, has_part, has_res, *refs):
+    acts, weights, rest, out_ref = refs[:n_pairs], refs[n_pairs:2 * n_pairs], list(refs[2 * n_pairs:-1]), refs[-1]
     total = None
     for act, weight in zip(acts, weights):
         for half in range(n_half):
             term = dot_nt(act[half], weight[half])
             total = term if total is None else total + term
+    if has_part:
+        total = total + rest.pop(0)[...].astype(F32)
     rounded = total.astype(BF16)
     if has_res:
-        rounded = (refs[2 * n_pairs][...].astype(F32) + rounded.astype(F32)).astype(BF16)
+        rounded = (rest.pop(0)[...].astype(F32) + rounded.astype(F32)).astype(BF16)
     out_ref[...] = rounded
 
 
-def project_back(acts, weights, res=None):
+def project_back(acts, weights, part=None, res=None):
     n_half, tokens, _ = acts[0].shape
     dim = weights[0].shape[1]
     bm, bn = min(1024, tokens), 512
     widths = [a.shape[2] for a in acts]
     out_spec = pl.BlockSpec((bm, bn), lambda m, n: (m, n))
+    extra = [v for v in (part, res) if v is not None]
     return pl.pallas_call(
-        functools.partial(gather_sum_kernel, len(acts), n_half, res is not None),
+        functools.partial(project_back_kernel, len(acts), n_half, part is not None, res is not None),
         grid=(tokens // bm, dim // bn),
         in_specs=[pl.BlockSpec((n_half, bm, w), lambda m, n: (0, m, 0)) for w in widths]
-        + [pl.BlockSpec((n_half, bn, w), lambda m, n: (0, n, 0)) for w in widths] + ([] if res is None else [out_spec]),
+        + [pl.BlockSpec((n_half, bn, w), lambda m, n: (0, n, 0)) for w in widths] + [out_spec] * len(extra),
         out_specs=out_spec,
         out_shape=jax.ShapeDtypeStruct((tokens, dim), BF16),
         compiler_params=pltpu.CompilerParams(dimension_semantics=("arbitrary", "arbitrary"), vmem_limit_bytes=VMEM_LIMIT),
         cost_estimate=cost(2 * tokens * dim * n_half * sum(widths), 2 * n_half * (tokens + 2 * dim) * sum(widths) + 4 * tokens * dim),
         name="project_back",
-    )(*acts, *weights, *([] if res is None else [res]))
+    )(*acts, *weights, *extra)
 
 
 def input_grad_kernel(x_ref, dy_ref, dh_ref, gain_ref, dx_ref, dgain_ref):
@@ -295,35 +305,60 @@
 
 def solution(mesh):
     tp = mesh.shape['tp']
-    everyone = ('tp', 'fsdp')
-    act_spec = P('fsdp', 'tp', None)
-    col_spec = P('fsdp', 'tp')
-    row_spec = P('tp', 'fsdp')
+    chips = mesh.shape['fsdp'] // CORES
+    step_mesh = Mesh(mesh.devices.reshape(tp, chips, CORES), ('tp', 'chip', 'core'))
+    across = ('tp', 'chip')
+    fsdp = ('chip', 'core')
+    act_spec = P(fsdp, 'tp', None)
+    col_spec = P(fsdp, 'tp')
+    row_spec = P('tp', fsdp)
 
     def shard_body(x_loc, gain, wq_loc, wk_loc, wv_loc, wo_loc, dy_loc):
         batch, seq, dim = x_loc.shape
         tokens = batch * seq
         q_cols, kv_cols = wq_loc.shape[1], wk_loc.shape[1]
-        tp_idx = lax.axis_index('tp')
-
-        def gather(block):
-            return lax.all_gather(block, everyone, axis=0, tiled=True).reshape(tp, dim, block.shape[1])
+        kw, qw = kv_cols // CORES, q_cols // CORES
+        rows = wq_loc.shape[0]
+        tp_idx, core = lax.axis_index('tp'), lax.axis_index('core')
+        first = core == 0
+
+        def swap(value):
+            return lax.ppermute(value, 'core', [(0, 1), (1, 0)])
+
+        def by_core(mine, other, axis):
+            return jnp.concatenate([jnp.where(first, mine, other), jnp.where(first, other, mine)], axis=axis)
+
+        def columns(block, width):
+            return (lax.dynamic_slice_in_dim(block, core * width, width, axis=1),
+                    lax.dynamic_slice_in_dim(block, (1 - core) * width, width, axis=1))
+
+        def gather(mine, other):
+            block = by_core(mine, swap(other), 0)
+            return lax.all_gather(block, across, axis=0, tiled=True).reshape(tp, dim, block.shape[1])
 
         def scatter(parts):
-            return lax.psum_scatter(parts.reshape(tp * dim, parts.shape[2]), everyone, scatter_dimension=0, tiled=True)
-
-        kw, qw = kv_cols // GROUPS, q_cols // GROUPS
-        wo_flipped = flip(wo_loc, GROUPS)
-        wkv, wq, wo = [], [], []
-        for g in range(GROUPS):
-            ks = slice(g * kw, (g + 1) * kw)
-            wkv.append(gather(jnp.concatenate([wk_loc[:, ks], wv_loc[:, ks]], axis=1)))
-            wq.append(gather(wq_loc[:, g * qw:(g + 1) * qw]))
-            wo.append(gather(wo_flipped[g]))
+            return lax.psum_scatter(parts.reshape(tp * dim, parts.shape[2]), across, scatter_dimension=0, tiled=True)
+
+        def settle(grad):
+            grad = grad.astype(BF16)
+            mine = lax.dynamic_slice_in_dim(grad, core * rows, rows)
+            other = swap(lax.dynamic_slice_in_dim(grad, (1 - core) * rows, rows))
+            return jnp.where(first, mine, other), jnp.where(first, other, mine)
 
         x = x_loc.reshape(tokens, dim)
         dy = dy_loc.reshape(tokens, dim)
+        k_mine, k_other = columns(wk_loc, kw)
+        v_mine, v_other = columns(wv_loc, kw)
+        wkv = gather(jnp.concatenate([k_mine, v_mine], axis=1), jnp.concatenate([k_other, v_other], axis=1))
+        wq = gather(*columns(wq_loc, qw))
+        flipped = flip(wo_loc, CORES)
+        wo = gather(jnp.where(first, flipped[0], flipped[1]), jnp.where(first, flipped[1], flipped[0]))
+
         normed, normed_t, dy_t = prepare(x, dy, gain)
+        acts = (normed, swap(normed))
+        d_outs = (dy, swap(dy))
+        acts_t = [normed_t, swap(normed_t)]
+        d_outs_t = [dy_t, swap(dy_t)]
 
         cos_tab, sin_tab = rope_tables(seq * tp)
         tables = jnp.stack([lax.dynamic_slice_in_dim(cos_tab, tp_idx * seq, seq), lax.dynamic_slice_in_dim(sin_tab, tp_idx * seq, seq),
@@ -334,51 +369,50 @@
             act = after(dep, act)
             return [dot_nn(act, weights[z]).astype(BF16) for z in range(tp)]
 
-        def attend_group(kv_g, kv_prev_g, q_g, d_mixed, dep):
-            return attend(seq, second, after(dep, tables), q_g, kv_g, d_mixed, kv_prev_g)
-
-        def send_kv(kv_g):
-            return [lax.ppermute(part, 'tp', [(0, 1)]) for part in kv_g]
+        def send_kv(kv):
+            return [lax.ppermute(part, 'tp', [(0, 1)]) for part in kv]
+
+        def attend_set(kv, kv_prev, q, d_mixed, dep):
+            return attend(seq, second, after(dep, tables), q, kv, d_mixed, kv_prev)
 
         def kv_grad(own, prev):
             return (own + lax.ppermute(prev, 'tp', [(1, 0)]).astype(F32)).astype(BF16)
 
-        assert GROUPS == 2
-        kv0 = project(normed, wkv[0], normed)
+        kv0 = project(acts[0], wkv, normed)
         prev0 = send_kv(kv0)
-        q0 = project(normed, wq[0], kv0[-1])
-        d_mixed0 = project(dy, wo[0], q0[-1])
-        kv1 = project(normed, wkv[1], d_mixed0[-1])
+        kv1 = project(acts[1], wkv, kv0[-1])
         prev1 = send_kv(kv1)
-        mixed0, d_q0, own0, back0 = attend_group(kv0, prev0, q0, d_mixed0, kv1[-1])
+        q0 = project(acts[0], wq, kv1[-1])
+        q1 = project(acts[1], wq, q0[-1])
+        d_mixed0 = project(d_outs[0], wo, q1[-1])
+        mixed0, d_q0, own0, back0 = attend_set(kv0, prev0, q0, d_mixed0, d_mixed0[-1])
         d_kv0 = kv_grad(own0, back0)
-        part = weight_grad(after(mixed0, dy_t), mixed0)
-        dwo0 = scatter(part)
-        part = weight_grad(after(part, normed_t), d_q0)
-        dwq0 = scatter(part)
-        q1 = project(normed, wq[1], part)
-        d_mixed1 = project(dy, wo[1], q1[-1])
-        mixed1, d_q1, own1, back1 = attend_group(kv1, prev1, q1, d_mixed1, d_mixed1[-1])
+        d_mixed1 = project(d_outs[1], wo, mixed0)
+        mixed1, d_q1, own1, back1 = attend_set(kv1, prev1, q1, d_mixed1, d_mixed1[-1])
         d_kv1 = kv_grad(own1, back1)
-        part = weight_grad(after(mixed1, normed_t), d_kv0)
-        dwkv0 = scatter(part)
-        part = weight_grad(after(part, dy_t), mixed1)
-        dwo1 = scatter(part)
-        part = weight_grad(after(part, normed_t), d_q1)
-        dwq1 = scatter(part)
-        y = project_back([mixed0, mixed1], wo, after(part, x))
-        part = weight_grad(after(y, normed_t), d_kv1)
-        dwkv1 = scatter(part)
-        d_normed = project_back([after(part, d_q0), d_q1, d_kv0, d_kv1], wq + wkv)
+
+        part = weight_grad([after(mixed1, d_outs_t[0]), d_outs_t[1]], [mixed0, mixed1])
+        dwo = scatter(part)
+        part = weight_grad([after(part, acts_t[0]), acts_t[1]], [d_q0, d_q1])
+        dwq = scatter(part)
+        part = weight_grad([after(part, acts_t[0]), acts_t[1]], [d_kv0, d_kv1])
+        dwkv = scatter(part)
+
+        y_other = project_back([after(part, mixed1)], [wo])
+        y_part = swap(y_other)
+        dh_other = project_back([after(y_other, d_q1), d_kv1], [wq, wkv])
+        dh_part = swap(dh_other)
+        y = project_back([after(dh_other, mixed0)], [wo], part=y_part, res=x)
+        d_normed = project_back([after(y, d_q0), d_kv0], [wq, wkv], part=dh_part)
         dx, d_gain = input_grad(x, dy, d_normed, gain)
-        d_gain = lax.psum(d_gain.reshape(dim), everyone)
-
-        dwo_loc = finish_flip([dwo0, dwo1])
-        dwq_loc, = finish([dwq0, dwq1], 1)
-        dwk_loc, dwv_loc = finish([dwkv0, dwkv1], 2)
+        d_gain = lax.psum(d_gain.reshape(dim), ('tp', 'chip', 'core'))
+
+        dwo_loc = finish_flip(settle(after(d_gain, dwo)))
+        dwq_loc, = finish(settle(after(d_gain, dwq)), 1)
+        dwk_loc, dwv_loc = finish(settle(after(d_gain, dwkv)), 2)
         return (y.reshape(x_loc.shape), dx.reshape(x_loc.shape), dwq_loc, dwk_loc, dwv_loc, dwo_loc, d_gain)
 
-    return jax.shard_map(shard_body, mesh=mesh,
+    return jax.shard_map(shard_body, mesh=step_mesh,
                          in_specs=(act_spec, P(), col_spec, col_spec, col_spec, row_spec, act_spec),
                          out_specs=(act_spec, act_spec, col_spec, col_spec, col_spec, row_spec, P()),
                          check_vma=False)

time: 1300 us -> 1140 us (0.88)
  waiting for transfers between devices: 635 us -> 452 us
  other arithmetic: 17.8 us -> 32.8 us
    reduce_scatter x6 -> x3, waiting for transfers between devices: 426 us -> 182 us  [scatter(): lax.psum_scatter(parts.reshape(tp * dim, parts.shape[2]), across, scatter...]
    ppermute x2, waiting for transfers between devices: 47.8 us -> 89.3 us  [kv_grad(): return (own + lax.ppermute(prev, 'tp', [(1, 0)]).astype(F32)).astype(BF16)]
    ppermute x4 -> x16, waiting for transfers between devices: 0.01 us -> 24.8 us  [the longest x12 19 us: swap(): return lax.ppermute(value, 'core', [(0, 1), (1, 0)])]
    all_gather x6 -> x3, waiting for transfers between devices: 158 us -> 155 us  [gather(): lax.all_gather(block, across, axis=0, tiled=True)]
    pallas_call x8 -> x7, Pallas kernels: 273 us -> 271 us  [the longest x4 143 us: project_back(): pl.pallas_call(functools.partial(project_back_kernel, len(acts), n_half,...]
  transfers between devices with their start and end apart: 18 -> 24, of which waited for: 9 -> 11; matrix products, arithmetic and copies ran while one was open for 13% -> 16% of each run, Pallas kernels for 30% -> 33%
where the time goes in v2:
time: 1140 us; the launch traced here: 1130 us
  waiting for transfers between devices  452 us (40%)
  Pallas kernels  408 us (36%)
  matrix products  161 us (14%)
  blocking collectives  33.3 us (3%)
  other arithmetic  32.8 us (3%)
  starting transfers between devices  21.7 us (2%)
  between operations  14.7 us (1%)
    reduce_scatter x3, waiting for transfers between devices, scatter(): lax.psum_scatter(parts.reshape(tp * dim, parts.shape[2]), across, scatter...  182 us
    dot_general x12, matrix products, dot_nn(): lax.dot_general(a, b, (((1,), (0,)), ((), ())), preferred_element_type=F32)  161 us
    all_gather x3, waiting for transfers between devices, gather(): lax.all_gather(block, across, axis=0, tiled=True)  155 us
    pallas_call x4, Pallas kernels, project_back(): pl.pallas_call(functools.partial(project_back_kernel, len(acts), n_half,...  143 us
    pallas_call x3, Pallas kernels, weight_grad(): pl.pallas_call(functools.partial(weight_grad_kernel, n_sets), grid=(n_hal...  129 us
    ppermute x2, waiting for transfers between devices, kv_grad(): return (own + lax.ppermute(prev, 'tp', [(1, 0)]).astype(F32)).astype(BF16)  89.3 us
    pallas_call x2, Pallas kernels, attend(): pl.pallas_call(functools.partial(attend_kernel, qw // kw, kw // HEAD_DIM,...  71.4 us
    psum x1, blocking collectives, shard_body(): d_gain = lax.psum(d_gain.reshape(dim), ('tp', 'chip', 'core'))  33.3 us
  transfers between devices with their start and end apart: 24, of which 11 were waited for; matrix products, arithmetic and copies ran while one was open for 16% of the time, Pallas kernels for 33%

profile of v2, /device:TPU:0, one launch (start us, length us, event | category | flops | bytes accessed | tf_op | source)
XLA Modules:
  0.0 1127.4 jit_solution(14103434950235059407)
XLA Ops:
  15.4 27.5 %prepare.1 = (bf16[2048,3072]{1,0:T(8,128)(2,1)}, bf16[3072,2048]{1,0:T(8,128)(2,1)}, bf16[3072,2048]{1,0:T(8,128)(2,1)}) custom-call(bf16[2048,3072]{1,0:T(8,128)(2,1)} %bitcast.33, bf16[2048,3072]{1,0:T(8,128)(2,1)} %bitcast.36, f32[1,3072]{1,0:T(1,128)} %bitcast.44), custom_call_target="tpu_custom_call" | custom-call | flops 377487360 | bytes 62914560 | tf_op jit(solution)/shard_map/prepare/pallas_call | solution.py:156
  47.1 16.0 %collective-permute-done.3 = bf16[384,768]{1,0:T(8,128)(2,1)S(1)} collective-permute-done((bf16[384,768]{1,0:T(8,128)(2,1)S(1)}, bf16[384,768]{1,0:T(8,128)(2,1)S(1)}, u32[]{:S(2)}, u32[]{:S(2)}) %collective-permute-start.3) | collective-permute-done | bytes 589856 | tf_op jit(solution)/shard_map/ppermute | solution.py:326
  75.1 13.0 %convolution_convert_fusion.1.refs_2_ = bf16[2048,512]{1,0:T(8,128)(2,1)} fusion(bf16[2048,3072]{1,0:T(8,128)(2,1)} %get-tuple-element.45, bf16[6144,512]{1,0:T(8,128)(2,1)} %all-gather.4.cloned.1.call-done), kind=kOutput, calls=%fused_computation.27 | convolution fusion | flops 6443499520 | bytes 17825792 | tf_op jit(solution)/shard_map/dot_general | solution.py:29
  92.8 10.6 convolution_convert_fusion.3.refs_3_
  106.6 9.6 convolution_convert_fusion.2.refs_3_
  116.2 11.3 %convolution_convert_fusion.refs_2_ = bf16[2048,512]{1,0:T(8,128)(2,1)} fusion(bf16[2048,3072]{1,0:T(8,128)(2,1)} %collective-permute-done.1, bf16[6144,512]{1,0:T(8,128)(2,1)S(1)} %copy-done.3), kind=kOutput, calls=%fused_computation.26 | convolution fusion | flops 6443499520 | bytes 17825792 | tf_op jit(solution)/shard_map/dot_general | solution.py:29
  127.5 82.8 %all-gather.6.cloned.1.call-done = bf16[6144,768]{1,0:T(8,128)(2,1)} async-done(((bf16[768,768]{1,0:T(8,128)(2,1)}), bf16[6144,768]{1,0:T(8,128)(2,1)}) %all-gather.6.cloned.1.call-update) | async-done | bytes 9437200 | tf_op jit(solution)/shard_map/all_gather | solution.py:337
  210.3 15.5 %fusion.16.refs_1_ = bf16[2048,768]{1,0:T(8,128)(2,1)} fusion(bf16[2048,3072]{1,0:T(8,128)(2,1)} %get-tuple-element.45, bf16[6144,768]{1,0:T(8,128)(2,1)} %all-gather.6.cloned.1.call-done), kind=kOutput, calls=%fused_computation.18 | convolution fusion | flops 9665249280 | bytes 20447232 | tf_op jit(solution)/shard_map/dot_general | solution.py:29
  225.9 14.0 %fusion.19.refs_1_ = bf16[2048,768]{1,0:T(8,128)(2,1)} fusion(bf16[2048,3072]{1,0:T(8,128)(2,1)} %collective-permute-done.1, bf16[6144,768]{1,0:T(8,128)(2,1)S(1)} %copy-done.2), kind=kOutput, calls=%fused_computation.19 | convolution fusion | flops 9665249280 | bytes 20447232 | tf_op jit(solution)/shard_map/dot_general | solution.py:29
  239.9 64.9 %all-gather.8.cloned.1.call-done = bf16[6144,768]{1,0:T(8,128)(2,1)} async-done(((bf16[768,768]{1,0:T(8,128)(2,1)}), bf16[6144,768]{1,0:T(8,128)(2,1)}) %all-gather.8.cloned.1.call-update) | async-done | bytes 9437200 | tf_op jit(solution)/shard_map/all_gather | solution.py:337
  304.8 15.7 %fusion.22.refs_5_ = bf16[2048,768]{1,0:T(8,128)(2,1)} fusion(bf16[2048,3072]{1,0:T(8,128)(2,1)} %bitcast.38, bf16[6144,768]{1,0:T(8,128)(2,1)} %all-gather.8.cloned.1.call-done), kind=kOutput, calls=%fused_computation.20 | convolution fusion | flops 9665249280 | bytes 20447232 | tf_op jit(solution)/shard_map/dot_general | solution.py:29
  320.5 15.5 %fusion.34.refs_4_ = bf16[2048,768]{1,0:T(8,128)(2,1)} fusion(bf16[2048,3072]{1,0:T(8,128)(2,1)} %bitcast.39, bf16[6144,768]{1,0:T(8,128)(2,1)} %all-gather.8.cloned.1.call-done), kind=kOutput, calls=%fused_computation.24 | convolution fusion | flops 9665249280 | bytes 20447232 | tf_op jit(solution)/shard_map/dot_general | solution.py:29
  336.1 11.3 fusion.28.refs_0_
  354.6 35.9 %attend.2 = (bf16[2,2048,768]{2,1,0:T(8,128)(2,1)}, bf16[2,2048,768]{2,1,0:T(8,128)(2,1)}, f32[2,2048,512]{2,1,0:T(8,128)}, bf16[2,2048,512]{2,1,0:T(8,128)(2,1)}) custom-call(s32[1]{0:T(128)} %bitcast.second_ref, f32[4,128,128]{2,1,0:T(8,128)} %pad_maximum_fusion.5.tab_ref, bf16[2048,768]{1,0:T(8,128)(2,1)} %fusion.28.refs_0_, ...), custom_call_target="tpu_custom_call" | custom-call | flops 38654705664 | bytes 39845888 | tf_op jit(solution)/shard_map/attend/pallas_call | solution.py:128
  390.6 15.5 %fusion.25.refs_5_ = bf16[2048,768]{1,0:T(8,128)(2,1)} fusion(bf16[2048,3072]{1,0:T(8,128)(2,1)} %collective-permute-done.6, bf16[6144,768]{1,0:T(8,128)(2,1)} %all-gather.8.cloned.1.call-done), kind=kOutput, calls=%fused_computation.21 | convolution fusion | flops 9665249280 | bytes 20447232 | tf_op jit(solution)/shard_map/dot_general | solution.py:29
  406.1 14.1 %fusion.37.refs_4_ = bf16[2048,768]{1,0:T(8,128)(2,1)} fusion(bf16[2048,3072]{1,0:T(8,128)(2,1)} %collective-permute-done.6, bf16[6144,768]{1,0:T(8,128)(2,1)S(1)} %bitcast.59), kind=kOutput, calls=%fused_computation.25 | convolution fusion | flops 9665249280 | bytes 20447232 | tf_op jit(solution)/shard_map/dot_general | solution.py:29
  420.2 14.5 %fusion.31.refs_0_ = bf16[2048,768]{1,0:T(8,128)(2,1)} fusion(bf16[2048,3072]{1,0:T(8,128)(2,1)} %collective-permute-done.1, bf16[6144,768]{1,0:T(8,128)(2,1)S(1)} %bitcast.55), kind=kOutput, calls=%fused_computation.23 | convolution fusion | flops 9665249280 | bytes 20447232 | tf_op jit(solution)/shard_map/dot_general | solution.py:29
  440.5 35.6 %attend.3 = (bf16[2,2048,768]{2,1,0:T(8,128)(2,1)}, bf16[2,2048,768]{2,1,0:T(8,128)(2,1)}, f32[2,2048,512]{2,1,0:T(8,128)}, bf16[2,2048,512]{2,1,0:T(8,128)(2,1)}) custom-call(s32[1]{0:T(128)} %bitcast.second_ref, f32[4,128,128]{2,1,0:T(8,128)} %pad_maximum_fusion.5.tab_ref, bf16[2048,768]{1,0:T(8,128)(2,1)} %fusion.31.refs_0_, ...), custom_call_target="tpu_custom_call" | custom-call | flops 38654705664 | bytes 39845888 | tf_op jit(solution)/shard_map/attend/pallas_call | solution.py:128
  478.7 47.2 %weight_grad.3 = f32[2,3072,768]{2,1,0:T(8,128)} custom-call(bf16[3072,2048]{1,0:T(8,128)(2,1)} %get-tuple-element.56.refs_0_, bf16[3072,2048]{1,0:T(8,128)(2,1)} %collective-permute-done.9.refs_1_, bf16[2,2048,768]{2,1,0:T(8,128)(2,1)} %get-tuple-element.68.refs_2_.refs_0_, bf16[2,2048,768]{2,1,0:T(8,128)(2,1)} %get-tuple-element.66.refs_3_.refs_0_), custom_call_target="tpu_custom_call" | custom-call | flops 38654705664 | bytes 81788928 | tf_op jit(solution)/shard_map/weight_grad/pallas_call | solution.py:181
  525.8 47.3 %weight_grad.4 = f32[2,3072,768]{2,1,0:T(8,128)} custom-call(bf16[3072,2048]{1,0:T(8,128)(2,1)} %get-tuple-element.61.refs_0_, bf16[3072,2048]{1,0:T(8,128)(2,1)} %collective-permute-done.10.refs_1_, bf16[2,2048,768]{2,1,0:T(8,128)(2,1)} %get-tuple-element.69.refs_2_.refs_0_, bf16[2,2048,768]{2,1,0:T(8,128)(2,1)} %get-tuple-element.67.refs_3_.refs_0_), custom_call_target="tpu_custom_call" | custom-call | flops 38654705664 | bytes 81788928 | tf_op jit(solution)/shard_map/weight_grad/pallas_call | solution.py:181
  573.1 9.2 collective-permute-done.12
  582.3 8.0 add_convert_fusion.refs_3_.refs_1_
  590.3 80.1 %collective-permute-done.11 = bf16[2,2048,512]{2,1,0:T(8,128)(2,1)S(1)} collective-permute-done((bf16[2,2048,512]{2,1,0:T(8,128)(2,1)}, bf16[2,2048,512]{2,1,0:T(8,128)(2,1)S(1)}, u32[]{:S(2)}, u32[]{:S(2)}) %collective-permute-start.11) | collective-permute-done | bytes 4194336 | tf_op jit(solution)/shard_map/ppermute | solution.py:379
  677.2 34.2 %weight_grad.5 = f32[2,3072,512]{2,1,0:T(8,128)} custom-call(bf16[3072,2048]{1,0:T(8,128)(2,1)} %get-tuple-element.61.refs_0_, bf16[3072,2048]{1,0:T(8,128)(2,1)} %collective-permute-done.10.refs_1_, bf16[2,2048,512]{2,1,0:T(8,128)(2,1)} %add_convert_fusion.1.refs_2_.refs_1_, bf16[2,2048,512]{2,1,0:T(8,128)(2,1)} %add_convert_fusion.refs_3_.refs_1_), custom_call_target="tpu_custom_call" | custom-call | flops 25769803776 | bytes 71303168 | tf_op jit(solution)/shard_map/weight_grad/pallas_call | solution.py:181
  712.6 27.3 %project_back.4 = bf16[2048,3072]{1,0:T(8,128)(2,1)} custom-call(bf16[2,2048,768]{2,1,0:T(8,128)(2,1)} %get-tuple-element.66.refs_3_.refs_0_, bf16[2,3072,768]{2,1,0:T(8,128)(2,1)} %bitcast.56), custom_call_target="tpu_custom_call" | custom-call | flops 19327352832 | bytes 50331648 | tf_op jit(solution)/shard_map/project_back/pallas_call | solution.py:216
  739.9 40.9 %project_back.5 = bf16[2048,3072]{1,0:T(8,128)(2,1)} custom-call(bf16[2,2048,768]{2,1,0:T(8,128)(2,1)} %get-tuple-element.67.refs_3_.refs_0_, bf16[2,2048,512]{2,1,0:T(8,128)(2,1)} %add_convert_fusion.refs_3_.refs_1_, bf16[2,3072,768]{2,1,0:T(8,128)(2,1)} %bitcast.50, bf16[2,3072,512]{2,1,0:T(8,128)(2,1)} %bitcast.60), custom_call_target="tpu_custom_call" | custom-call | flops 32212254720 | bytes 67108864 | tf_op jit(solution)/shard_map/project_back/pallas_call | solution.py:216
  781.3 32.7 %project_back.6 = bf16[2048,3072]{1,0:T(8,128)(2,1)} custom-call(bf16[2,2048,768]{2,1,0:T(8,128)(2,1)} %get-tuple-element.68.refs_2_.refs_0_, bf16[2,3072,768]{2,1,0:T(8,128)(2,1)} %bitcast.57, bf16[2048,3072]{1,0:T(8,128)(2,1)} %collective-permute-done.13.refs_2_, bf16[2048,3072]{1,0:T(8,128)(2,1)} %bitcast.34), custom_call_target="tpu_custom_call" | custom-call | flops 19327352832 | bytes 50331648 | tf_op jit(solution)/shard_map/project_back/pallas_call | solution.py:216
  814.0 41.8 %project_back.7.dh_ref = bf16[2048,3072]{1,0:T(8,128)(2,1)} custom-call(bf16[2,2048,768]{2,1,0:T(8,128)(2,1)} %get-tuple-element.69.refs_2_.refs_0_, bf16[2,2048,512]{2,1,0:T(8,128)(2,1)} %add_convert_fusion.1.refs_2_.refs_1_, bf16[2,3072,768]{2,1,0:T(8,128)(2,1)} %bitcast.51, bf16[2,3072,512]{2,1,0:T(8,128)(2,1)} %bitcast.61, ...), custom_call_target="tpu_custom_call" | custom-call | flops 32212254720 | bytes 67108864 | tf_op jit(solution)/shard_map/project_back/pallas_call | solution.py:216
  855.8 28.6 %input_grad.1 = (bf16[2048,3072]{1,0:T(8,128)(2,1)}, f32[1,3072]{1,0:T(1,128)}) custom-call(bf16[2048,3072]{1,0:T(8,128)(2,1)} %bitcast.35, bf16[2048,3072]{1,0:T(8,128)(2,1)} %bitcast.40, bf16[2048,3072]{1,0:T(8,128)(2,1)} %project_back.7.dh_ref, f32[1,3072]{1,0:T(1,128)} %bitcast.45), custom_call_target="tpu_custom_call" | custom-call | flops 377487360 | bytes 50331648 | tf_op jit(solution)/shard_map/input_grad/pallas_call | solution.py:249
  884.4 33.3 %psum.7 = f32[3072]{0:T(1024)} all-reduce(f32[3072]{0:T(1024)} %bitcast.46), channel_id=1, replica_groups=mesh['tp'=2,'chip'=4,'core'=2] {'tp','chip','core'}, use_global_device_ids=true, to_apply=%region_0.1 | all-reduce | flops 3072 | bytes 24576 | tf_op jit(solution)/shard_map/psum | solution.py:408
  920.5 39.2 %reduce-scatter.8.cloned.1.call-done = f32[768,768]{1,0:T(8,128)} async-done(((f32[6144,768]{1,0:T(8,128)}), f32[768,768]{1,0:T(8,128)}) %reduce-scatter.8.cloned.1.call-update) | async-done | bytes 2359312 | tf_op jit(solution)/shard_map/reduce_scatter | solution.py:340
  962.3 142.6 %reduce-scatter.4.cloned.1.call-done = f32[768,768]{1,0:T(8,128)} async-done(((f32[6144,768]{1,0:T(8,128)}), f32[768,768]{1,0:T(8,128)}) %reduce-scatter.4.cloned.1.call-update) | async-done | bytes 2359312 | tf_op jit(solution)/shard_map/reduce_scatter | solution.py:340
  (112 shorter events, 77.1 us)
Async XLA Ops:
  7.2 67.9 %all-gather.4.cloned.1.call-start = ((), (), s32[]{:S(2)}) async-start(), calls=%async_computation.3 | async-start | bytes 7077888 | tf_op jit(solution)/shard_map/all_gather | solution.py:337
  8.6 2.1 collective-permute-start
  11.8 198.5 %all-gather.6.cloned.1.call-start = ((), (), s32[]{:S(2)}) async-start(), calls=%async_computation.4 | async-start | bytes 10616832 | tf_op jit(solution)/shard_map/all_gather | solution.py:337
  12.0 2.0 collective-permute-start.2
  15.4 289.4 %all-gather.8.cloned.1.call-start = ((), (), s32[]{:S(2)}) async-start(), calls=%async_computation.5 | async-start | bytes 10616832 | tf_op jit(solution)/shard_map/all_gather | solution.py:337
  42.9 60.5 %collective-permute-start.1 = (bf16[2048,3072]{1,0:T(8,128)(2,1)}, bf16[2048,3072]{1,0:T(8,128)(2,1)}, u32[]{:S(2)}, u32[]{:S(2)}) collective-permute-start(bf16[2048,3072]{1,0:T(8,128)(2,1)} %get-tuple-element.45), channel_id=1, source_target_pairs={{0,1},{1,0},{2,3},{3,2},{4,5},{5,4},{6,7},{7,6},{8,9},{9,8},{10,11... | collective-permute-start | bytes 37748744 | tf_op jit(solution)/shard_map/ppermute | solution.py:326
  46.9 16.2 %collective-permute-start.3 = (bf16[384,768]{1,0:T(8,128)(2,1)S(1)}, bf16[384,768]{1,0:T(8,128)(2,1)S(1)}, u32[]{:S(2)}, u32[]{:S(2)}) collective-permute-start(bf16[384,768]{1,0:T(8,128)(2,1)S(1)} %broadcast_select_fusion.6), channel_id=1, source_target_pairs={{0,1},{1,0},{2,3},{3,2},{4,5},{5,4},{6,7},{7,6},{8,9},{9,8},{10,11... | collective-permute-start | bytes 1769480 | tf_op jit(solution)/shard_map/ppermute | solution.py:326
  65.4 852.3 %reduce-scatter.6.cloned.1.call-start = ((), (), s32[]{:S(2)}) async-start(), calls=%async_computation.7 | async-start | bytes 14155776 | tf_op jit(solution)/shard_map/reduce_scatter | solution.py:340
  65.5 325.0 %collective-permute-start.6 = (bf16[2048,3072]{1,0:T(8,128)(2,1)}, bf16[2048,3072]{1,0:T(8,128)(2,1)}, u32[]{:S(2)}, u32[]{:S(2)}) collective-permute-start(bf16[2048,3072]{1,0:T(8,128)(2,1)} %bitcast.37), channel_id=1, source_target_pairs={{0,1},{1,0},{2,3},{3,2},{4,5},{5,4},{6,7},{7,6},{8,9},{9,8},{10,11... | collective-permute-start | bytes 37748744 | tf_op jit(solution)/shard_map/ppermute | solution.py:326
  65.9 412.8 %collective-permute-start.9 = (bf16[3072,2048]{1,0:T(8,128)(2,1)}, bf16[3072,2048]{1,0:T(8,128)(2,1)}, u32[]{:S(2)}, u32[]{:S(2)}) collective-permute-start(bf16[3072,2048]{1,0:T(8,128)(2,1)} %get-tuple-element.56.refs_0_), channel_id=1, source_target_pairs={{0,1},{1,0},{2,3},{3,2},{4,5},{5,4},{6,7},{7,6},{8,9},{9,8},{10,11... | collective-permute-start | bytes 37748744 | tf_op jit(solution)/shard_map/ppermute | solution.py:326
  66.0 459.8 %collective-permute-start.10 = (bf16[3072,2048]{1,0:T(8,128)(2,1)}, bf16[3072,2048]{1,0:T(8,128)(2,1)}, u32[]{:S(2)}, u32[]{:S(2)}) collective-permute-start(bf16[3072,2048]{1,0:T(8,128)(2,1)} %get-tuple-element.61.refs_0_), channel_id=1, source_target_pairs={{0,1},{1,0},{2,3},{3,2},{4,5},{5,4},{6,7},{7,6},{8,9},{9,8},{10,11... | collective-permute-start | bytes 37748744 | tf_op jit(solution)/shard_map/ppermute | solution.py:326
  88.1 259.2 %collective-permute-start.4 = (bf16[2048,512]{1,0:T(8,128)(2,1)}, bf16[2048,512]{1,0:T(8,128)(2,1)}, u32[]{:S(2)}, u32[]{:S(2)}) collective-permute-start(bf16[2048,512]{1,0:T(8,128)(2,1)} %convolution_convert_fusion.1.refs_2_), channel_id=1, source_target_pairs={{0,8},{1,9},{2,10},{3,11},{4,12},{5,13},{6,14},{7,15}} | collective-permute-start | bytes 6291464 | tf_op jit(solution)/shard_map/ppermute | solution.py:373
  103.4 248.6 %collective-permute-start.5 = (bf16[2048,512]{1,0:T(8,128)(2,1)}, bf16[2048,512]{1,0:T(8,128)(2,1)}, u32[]{:S(2)}, u32[]{:S(2)}) collective-permute-start(bf16[2048,512]{1,0:T(8,128)(2,1)} %convolution_convert_fusion.3.refs_3_), channel_id=1, source_target_pairs={{0,8},{1,9},{2,10},{3,11},{4,12},{5,13},{6,14},{7,15}} | collective-permute-start | bytes 6291464 | tf_op jit(solution)/shard_map/ppermute | solution.py:373
  116.2 231.2 %copy-start.4 = (bf16[2048,512]{1,0:T(8,128)(2,1)}, bf16[2048,512]{1,0:T(8,128)(2,1)S(1)}, u32[]{:S(2)}) copy-start(bf16[2048,512]{1,0:T(8,128)(2,1)S(1)} %convolution_convert_fusion.2.refs_3_) | copy-start | bytes 6291460
  304.8 31.2 %slice-start = ((s8[12582912]{0:T(1024)(128)(4,1)}), s8[4194304]{0:T(1024)(128)(4,1)S(1)}, s32[]{:S(2)}) async-start(s8[12582912]{0:T(1024)(128)(4,1)} %bitcast.47), calls=%async_computation.9 | async-start | bytes 8388608
  304.8 31.2 %slice-start.1 = ((s8[12582912]{0:T(1024)(128)(4,1)}), s8[4194304]{0:T(1024)(128)(4,1)S(1)}, s32[]{:S(2)}) async-start(s8[12582912]{0:T(1024)(128)(4,1)} %bitcast.47), calls=%async_computation.10 | async-start | bytes 8388608
  304.8 31.2 %slice-start.3 = ((s8[9437184]{0:T(1024)(128)(4,1)}), s8[4194304]{0:T(1024)(128)(4,1)S(1)}, s32[]{:S(2)}) async-start(s8[9437184]{0:T(1024)(128)(4,1)} %bitcast.52), calls=%async_computation.12 | async-start | bytes 8388608
  304.8 31.2 %slice-start.4 = ((s8[9437184]{0:T(1024)(128)(4,1)}), s8[4194304]{0:T(1024)(128)(4,1)S(1)}, s32[]{:S(2)}) async-start(s8[9437184]{0:T(1024)(128)(4,1)} %bitcast.52), calls=%async_computation.13 | async-start | bytes 8388608
  347.4 93.1 %collective-permute-start.8 = (bf16[2048,512]{1,0:T(8,128)(2,1)S(1)}, bf16[2048,512]{1,0:T(8,128)(2,1)}, u32[]{:S(2)}, u32[]{:S(2)}) collective-permute-start(bf16[2048,512]{1,0:T(8,128)(2,1)S(1)} %convolution_convert_fusion.2.refs_3_), channel_id=1, source_target_pairs={{0,8},{1,9},{2,10},{3,11},{4,12},{5,13},{6,14},{7,15}} | collective-permute-start | bytes 6291464 | tf_op jit(solution)/shard_map/ppermute | solution.py:373
  352.0 88.5 %collective-permute-start.7 = (bf16[2048,512]{1,0:T(8,128)(2,1)}, bf16[2048,512]{1,0:T(8,128)(2,1)}, u32[]{:S(2)}, u32[]{:S(2)}) collective-permute-start(bf16[2048,512]{1,0:T(8,128)(2,1)} %convolution_convert_fusion.refs_2_), channel_id=1, source_target_pairs={{0,8},{1,9},{2,10},{3,11},{4,12},{5,13},{6,14},{7,15}} | collective-permute-start | bytes 6291464 | tf_op jit(solution)/shard_map/ppermute | solution.py:373
  354.6 51.5 %slice-start.9 = ((s8[9437184]{0:T(1024)(128)(4,1)}), s8[1048576]{0:T(1024)(128)(4,1)S(1)}, s32[]{:S(2)}) async-start(s8[9437184]{0:T(1024)(128)(4,1)} %bitcast.58), calls=%async_computation.18 | async-start | bytes 2097152
  354.6 51.5 %slice-start.10 = ((s8[9437184]{0:T(1024)(128)(4,1)}), s8[4194304]{0:T(1024)(128)(4,1)S(1)}, s32[]{:S(2)}) async-start(s8[9437184]{0:T(1024)(128)(4,1)} %bitcast.58), calls=%async_computation.19 | async-start | bytes 8388608
  390.5 29.7 %slice-start.6 = ((s8[9437184]{0:T(1024)(128)(4,1)}), s8[4194304]{0:T(1024)(128)(4,1)S(1)}, s32[]{:S(2)}) async-start(s8[9437184]{0:T(1024)(128)(4,1)} %bitcast.54), calls=%async_computation.15 | async-start | bytes 8388608
  476.0 106.2 %collective-permute-start.12 = (bf16[2,2048,512]{2,1,0:T(8,128)(2,1)}, bf16[2,2048,512]{2,1,0:T(8,128)(2,1)}, u32[]{:S(2)}, u32[]{:S(2)}) collective-permute-start(bf16[2,2048,512]{2,1,0:T(8,128)(2,1)} %get-tuple-element.65), channel_id=1, source_target_pairs={{8,0},{9,1},{10,2},{11,3},{12,4},{13,5},{14,6},{15,7}} | collective-permute-start | bytes 12582920 | tf_op jit(solution)/shard_map/ppermute | solution.py:379
  477.3 193.0 %collective-permute-start.11 = (bf16[2,2048,512]{2,1,0:T(8,128)(2,1)}, bf16[2,2048,512]{2,1,0:T(8,128)(2,1)S(1)}, u32[]{:S(2)}, u32[]{:S(2)}) collective-permute-start(bf16[2,2048,512]{2,1,0:T(8,128)(2,1)} %get-tuple-element.63), channel_id=1, source_target_pairs={{8,0},{9,1},{10,2},{11,3},{12,4},{13,5},{14,6},{15,7}} | collective-permute-start | bytes 12582920 | tf_op jit(solution)/shard_map/ppermute | solution.py:379
  711.4 248.3 %reduce-scatter.8.cloned.1.call-start = ((), (), s32[]{:S(2)}) async-start(), calls=%async_computation.8 | async-start | bytes 21233664 | tf_op jit(solution)/shard_map/reduce_scatter | solution.py:340
  712.0 393.0 %reduce-scatter.4.cloned.1.call-start = ((), (), s32[]{:S(2)}) async-start(), calls=%async_computation.6 | async-start | bytes 21233664 | tf_op jit(solution)/shard_map/reduce_scatter | solution.py:340
  739.9 41.4 %collective-permute-start.13 = (bf16[2048,3072]{1,0:T(8,128)(2,1)}, bf16[2048,3072]{1,0:T(8,128)(2,1)}, u32[]{:S(2)}, u32[]{:S(2)}) collective-permute-start(bf16[2048,3072]{1,0:T(8,128)(2,1)} %project_back.4), channel_id=1, source_target_pairs={{0,1},{1,0},{2,3},{3,2},{4,5},{5,4},{6,7},{7,6},{8,9},{9,8},{10,11... | collective-permute-start | bytes 37748744 | tf_op jit(solution)/shard_map/ppermute | solution.py:326
  780.7 33.3 %collective-permute-start.14 = (bf16[2048,3072]{1,0:T(8,128)(2,1)}, bf16[2048,3072]{1,0:T(8,128)(2,1)}, u32[]{:S(2)}, u32[]{:S(2)}) collective-permute-start(bf16[2048,3072]{1,0:T(8,128)(2,1)} %project_back.5), channel_id=1, source_target_pairs={{0,1},{1,0},{2,3},{3,2},{4,5},{5,4},{6,7},{7,6},{8,9},{9,8},{10,11... | collective-permute-start | bytes 37748744 | tf_op jit(solution)/shard_map/ppermute | solution.py:326
  920.0 187.7 %collective-permute-start.16 = (bf16[384,512]{1,0:T(8,128)(2,1)}, bf16[384,512]{1,0:T(8,128)(2,1)S(1)}, u32[]{:S(2)}, u32[]{:S(2)}) collective-permute-start(bf16[384,512]{1,0:T(8,128)(2,1)} %constant_dynamic-slice_fusion.1), channel_id=1, source_target_pairs={{0,1},{1,0},{2,3},{3,2},{4,5},{5,4},{6,7},{7,6},{8,9},{9,8},{10,11... | collective-permute-start | bytes 1179656 | tf_op jit(solution)/shard_map/ppermute | solution.py:326
  962.3 148.4 %collective-permute-start.17 = (bf16[384,768]{1,0:T(8,128)(2,1)}, bf16[384,768]{1,0:T(8,128)(2,1)}, u32[]{:S(2)}, u32[]{:S(2)}) collective-permute-start(bf16[384,768]{1,0:T(8,128)(2,1)} %constant_dynamic-slice_fusion), channel_id=1, source_target_pairs={{0,1},{1,0},{2,3},{3,2},{4,5},{5,4},{6,7},{7,6},{8,9},{9,8},{10,11... | collective-permute-start | bytes 1769480 | tf_op jit(solution)/shard_map/ppermute | solution.py:326
  1107.6 8.0 collective-permute-start.15
  (9 other events, 152.0 us)
Sparse Core Ops, SparseCore 0:
  12.0 63.0 all-gather.3
  77.8 132.4 all-gather.5
  213.1 91.6 all-gather.7
  711.5 101.4 reduce-scatter.5
  817.2 142.4 reduce-scatter.7
  963.9 141.0 reduce-scatter.3
